TPU v7x, 128 devices: a whole 4x4x4 slice. The times are simulated.
128 devices in a mesh: grp: 2 (over core), dp: 64 (over y, x, z).
Axes of the slice: x: 4, y: 4, z: 4, core: 2. Of those that a mesh axis runs over, the one named last changes fastest.
Arguments:
- grad: bfloat16 [2, 32768, 8192], P('grp', None, 'dp'), may hold values from -40 to 40
- residual: bfloat16 [2, 32768, 8192], P('grp', None, 'dp'), may hold values from -4 to 4
- q_prev: float32 [5, 4, 8192], P(None, None, 'dp'), may hold values from -0.0625 to 0.0625
- owner_table: int32 [5], replicated, may hold values from 0 to 63, as said below
Outputs:
- new_residual: bfloat16 [2, 32768, 8192], P('grp', None, 'dp')
- q_new: float32 [5, 4, 8192], P(None, None, 'dp')
- owned: float32 [64, 4, 14336], P('dp')
Inputs may be any that keep to these rules, and one draw needn't show every extreme that they name: `owner_table`: the 5 owners are distinct.
All inputs are finite; a program needn't handle non-finite values.
Results may differ from a plain program's by a relative error of at most 0.0055.
Values sent between devices are 32-bit elements; how exact they have to be, the bound alone decides.
No kernel may reach another device: no remote copies, remote signals or barrier semaphores. Data moves between devices by JAX's collectives and lax.ppermute only.
A program may use at most 128 MiB of HBM per device.

v0:
```python
import jax
import jax.numpy as jnp
from jax import lax
from jax.sharding import PartitionSpec as P

D = 8192
KV = 1024
FF_WIN = 14336


EPSILON = 1e-06


def in_blocks(x, dim, count):
    before, after = (x.shape[:dim], x.shape[dim + 1 :])
    return jnp.moveaxis(x.reshape(*before, count, -1, *after), dim, 0)


def sent_and_summed(x, axis, dim):
    tiles = in_blocks(x, dim, lax.axis_size(axis))
    arrived = lax.all_to_all(tiles, axis, split_axis=0, concat_axis=0, tiled=True)
    return arrived.sum(axis=0)


def sent_to_all(x, axis):
    count = lax.axis_size(axis)
    return lax.all_to_all(jnp.broadcast_to(x[None], (count, *x.shape)), axis, 0, 0, tiled=True)


def taken_together(x, axis):
    return sent_to_all(x, axis).sum(axis=0)


def joined_along(tiles, dim):
    tiles = jnp.moveaxis(tiles, 0, dim)
    dims = tiles.shape
    return tiles.reshape(*dims[:dim], dims[dim] * dims[dim + 1], *dims[dim + 2 :])


def gather_directly(x, axis, dim):
    return joined_along(sent_to_all(x, axis), dim)


def block_sizes():
    return [D, KV, KV, D, FF_WIN]


def whiten(lower_factor, projected):
    solved = []
    for i in range(projected.shape[-2]):
        running = projected[..., i, :]
        for k in range(i):
            running = running - lower_factor[..., i, k, None] * solved[k]
        solved.append(running / lower_factor[..., i, i, None])
    return jnp.stack(solved, axis=-2)


def orthonormal(projected):
    gram_matrix = jnp.dot(projected, projected.T)
    gram_matrix = gram_matrix + EPSILON * jnp.eye(projected.shape[0], dtype=jnp.float32)
    return whiten(jnp.linalg.cholesky(gram_matrix), projected)


def body(grad, residual, q_prev, owner_table):
    group_count = lax.axis_size("grp")
    own_index = lax.axis_index("dp")
    sizes_list = block_sizes()
    slot_width = max(sizes_list)
    compensated = (grad[0].astype(jnp.float32) + residual[0].astype(jnp.float32)).astype(
        jnp.bfloat16
    )
    q_rounded = q_prev.astype(jnp.bfloat16)
    offsets = []
    pieces = []
    offset = 0
    for layer_id, count in enumerate(sizes_list):
        offsets.append(offset)
        pieces.append(
            lax.dot_general(
                q_rounded[layer_id],
                compensated[offset : offset + count],
                (((1,), (1,)), ((), ())),
                preferred_element_type=jnp.float32,
            )
        )
        offset += count
    rank_count = q_prev.shape[1]
    partial_value = jnp.concatenate(pieces, axis=1)
    share = sent_and_summed(partial_value, "dp", 1)
    share = taken_together(share, "grp") / group_count
    summed = gather_directly(share, "dp", 1)
    bases = []
    owned = jnp.zeros((1, rank_count, slot_width), jnp.float32)
    for layer_id, count in enumerate(sizes_list):
        projected = summed[:, offsets[layer_id] : offsets[layer_id] + count]
        padded = jnp.pad(projected, ((0, 0), (0, slot_width - count)))
        is_owner = (owner_table[layer_id] == own_index).astype(jnp.float32)
        owned = owned + is_owner * padded[None]
        bases.append(orthonormal(projected).astype(jnp.bfloat16))
    q_parts = []
    for layer_id, count in enumerate(sizes_list):
        start_row = offsets[layer_id]
        q_parts.append(
            jnp.dot(
                bases[layer_id],
                compensated[start_row : start_row + count],
                preferred_element_type=jnp.float32,
            )
        )
    q_new = taken_together(jnp.stack(q_parts), "grp") / group_count
    q_round = q_new.astype(jnp.bfloat16)
    residuals = []
    for layer_id, count in enumerate(sizes_list):
        start_row = offsets[layer_id]
        update = lax.dot_general(
            bases[layer_id],
            q_round[layer_id],
            (((0,), (0,)), ((), ())),
            preferred_element_type=jnp.float32,
        )
        residuals.append(
            (compensated[start_row : start_row + count].astype(jnp.float32) - update).astype(
                jnp.bfloat16
            )
        )
    return (jnp.concatenate(residuals, axis=0)[None], q_new, owned)


def solution(mesh):
    in_specs = (P("grp", None, "dp"), P("grp", None, "dp"), P(None, None, "dp"), P())
    out_specs = (P("grp", None, "dp"), P(None, None, "dp"), P("dp", None, None))
    return jax.shard_map(body, mesh=mesh, in_specs=in_specs, out_specs=out_specs, check_vma=False)
```

profile of v0, /device:TPU:1, one launch (start us, length us, event | category | flops | bytes accessed | tf_op | source)
XLA Modules:
  0.0 136.7 jit_solution(7236228563948141355)
XLA Ops:
  0.6 0.7 convert_element_type.83
  1.3 7.0 %add_convert_fusion = bf16[1,32768,128]{2,1,0:T(8,128)(2,1)S(1)} fusion(bf16[1,32768,128]{2,1,0:T(8,128)(2,1)} %param.6, bf16[1,32768,128]{2,1,0:T(8,128)(2,1)} %param.5), kind=kLoop, calls=%fused_computation.3 | loop fusion | flops 16777216 | bytes 25165824 | tf_op jit(solution)/shard_map/convert_element_type | solution.py:69
  8.4 0.6 fusion.8
  9.0 0.2 fusion.17
  9.2 0.2 fusion.16
  9.4 0.7 fusion.7
  10.1 1.7 %copy-done = bf16[1,32768,128]{2,1,0:T(8,128)(2,1)} copy-done((bf16[1,32768,128]{2,1,0:T(8,128)(2,1)}, bf16[1,32768,128]{2,1,0:T(8,128)(2,1)S(1)}, u32[]{:S(2)}) %copy-start) | copy-done | bytes 8388632
  11.8 1.1 fusion.2
  12.8 23.7 %all_to_all.20 = f32[64,4,512]{2,1,0:T(4,128)S(1)} all-to-all(f32[64,4,512]{2,1,0:T(4,128)S(1)} %bitcast.216), channel_id=1, replica_groups=mesh['grp'=2,'dp'=64] {'dp'}, dimensions={0} | all-to-all | bytes 1048576 | tf_op jit(solution)/shard_map/all_to_all | solution.py:21
  36.6 5.7 %all_to_all.21 = f32[2,4,512]{2,1,0:T(4,128)S(1)} all-to-all(f32[2,4,512]{2,1,0:T(4,128)S(1)} %broadcast_in_dim.8), channel_id=1, replica_groups=mesh['grp'=2,'dp'=64] {'grp'}, dimensions={0} | all-to-all | bytes 32768 | tf_op jit(solution)/shard_map/all_to_all | solution.py:27
  42.3 0.9 broadcast_in_dim.9
  43.2 4.6 %all-to-all-start.2 = ((f32[64,4,512]{2,1,0:T(4,128)}), f32[64,4,512]{2,1,0:T(4,128)S(1)}, u32[]{:S(2)}, u32[]{:S(2)}) async-start(f32[64,4,512]{2,1,0:T(4,128)} %broadcast_in_dim.9), calls=%async_computation.2 | async-start | bytes 1048576 | tf_op jit(solution)/shard_map/all_to_all | solution.py:27
  47.8 0.7 fusion.99
  51.7 8.5 %all-to-all-done.2 = f32[64,4,512]{2,1,0:T(4,128)S(1)} async-done(((f32[64,4,512]{2,1,0:T(4,128)}), f32[64,4,512]{2,1,0:T(4,128)S(1)}, u32[]{:S(2)}, u32[]{:S(2)}) %all-to-all-start.2) | async-done | bytes 524320 | tf_op jit(solution)/shard_map/all_to_all | solution.py:27
  60.2 0.2 convolution_add_fusion.4
  60.4 0.2 convolution_add_fusion
  60.6 0.1 convolution_add_fusion.2
  60.8 0.2 convolution_add_fusion.3
  61.1 0.4 cholesky.89
  61.5 0.6 compare_reduce_fusion.4
  62.1 0.6 select_select_fusion.4
  62.9 0.4 cholesky.111
  63.3 0.6 compare_reduce_fusion.2
  63.9 0.6 select_select_fusion.2
  64.7 0.4 cholesky.100
  65.1 0.6 compare_reduce_fusion.3
  65.7 0.6 select_select_fusion.3
  66.5 0.4 cholesky.122
  66.9 0.6 compare_reduce_fusion.1
  67.5 0.6 select_select_fusion.1
  68.3 0.4 cholesky.133
  68.7 0.6 compare_reduce_fusion
  69.3 0.6 select_select_fusion
  70.0 0.7 fusion.94
  70.7 0.7 fusion.95
  71.4 0.7 fusion.97
  72.1 0.7 fusion.96
  72.7 0.7 fusion.98
  73.4 0.8 fusion.68
  74.2 1.2 fusion.78
  75.4 1.2 fusion.73
  76.6 1.4 %fusion.69 = (bf16[1,14336]{1,0:T(2,128)(2,1)S(1)}, f32[1,14336]{1,0:T(1,128)S(1)}) fusion(f32[]{:T(128)} %bitcast.71, f32[1,14336]{1,0:T(1,128)S(1)} %get-tuple-element.7, f32[]{:T(128)} %bitcast.70, f32[4,32768]{1,0:T(4,128)S(1)} %bitcast.206), kind=kLoop, calls=%fused_computation.158 | loop fusion | flops 57344 | bytes 200712 | tf_op jit(solution)/shard_map/convert.1
  78.0 2.0 %fusion.71 = (bf16[1,14336]{1,0:T(2,128)(2,1)S(1)}, f32[1,14336]{1,0:T(1,128)S(1)}) fusion(f32[]{:T(128)} %bitcast.74, f32[1,14336]{1,0:T(1,128)S(1)} %get-tuple-element.9, f32[]{:T(128)} %bitcast.73, f32[1,14336]{1,0:T(1,128)S(1)} %get-tuple-element.7, f32[]{:T(128)} %bitcast.72, f32[4,32768]{1,0:T(4,128)S(1)} %bitcast.207), kind=kLoop, calls=%fused_computation.159 | loop fusion | flops 86016 | bytes 258060 | tf_op jit(solution)/shard_map/convert.2
  80.0 2.6 %fusion.74 = (bf16[1,8192]{1,0:T(2,128)(2,1)S(1)}, f32[1,8192]{1,0:T(1,128)S(1)}, bf16[1,8192]{1,0:T(2,128)(2,1)S(1)}, f32[1,8192]{1,0:T(1,128)S(1)}) fusion(f32[]{:T(128)} %bitcast.59, f32[1,8192]{1,0:T(1,128)S(1)} %get-tuple-element.13, f32[]{:T(128)} %bitcast.58, f32[4,32768]{1,0:T(4,128)S(1)} %bitcast.208, f32[]{:T(128)} %bitcast.23, ...), kind=kLoop, calls=%fused_computation.161 | loop fusion | flops 65536 | bytes 229392 | tf_op jit(solution)/shard_map/convert.5
  82.7 3.9 %fusion.76 = (bf16[1,8192]{1,0:T(2,128)(2,1)S(1)}, f32[1,8192]{1,0:T(1,128)S(1)}, bf16[1,8192]{1,0:T(2,128)(2,1)S(1)}, f32[1,8192]{1,0:T(1,128)S(1)}) fusion(f32[]{:T(128)} %bitcast.62, f32[1,8192]{1,0:T(1,128)S(1)} %get-tuple-element.15, f32[]{:T(128)} %bitcast.61, f32[1,8192]{1,0:T(1,128)S(1)} %get-tuple-element.13, f32[]{:T(128)} %bitcast.60, ...), kind=kLoop, calls=%fused_computation.162 | loop fusion | flops 98304 | bytes 294936 | tf_op jit(solution)/shard_map/convert.6
  86.6 5.3 %divide_convert_fusion.1 = (bf16[1,8192]{1,0:T(2,128)(2,1)S(1)}, bf16[1,8192]{1,0:T(2,128)(2,1)S(1)}) fusion(f32[1,8192]{1,0:T(1,128)S(1)} %get-tuple-element.17, f32[1,8192]{1,0:T(1,128)S(1)} %get-tuple-element.15, f32[1,8192]{1,0:T(1,128)S(1)} %get-tuple-element.13, f32[4,32768]{1,0:T(4,128)S(1)} %bitcast.210, f32[]{:T(128)} %bitcast.66, f32[]{:T(128)} %bitcast.65, ...), kind=kLoop, calls=%fused_computation.87 | loop fusion | flops 131072 | bytes 294944 | tf_op jit(solution)/shard_map/convert.7
  91.8 2.0 %fusion.21 = f32[5,4,128]{2,1,0:T(4,128)S(1)} fusion(bf16[1,32768,128]{2,1,0:T(8,128)(2,1)} %copy-done, bf16[1,8192]{1,0:T(2,128)(2,1)S(1)} %get-tuple-element.39, bf16[1,8192]{1,0:T(2,128)(2,1)S(1)} %get-tuple-element.40, bf16[1,8192]{1,0:T(2,128)(2,1)S(1)} %get-tuple-element.42, bf16[1,8192]{1,0:T(2,128)(2,1)S(1)} %get-tuple-element.44), kind=kOutput, calls=%fused_computation.35 | convolution fusion | flops 8650751 | bytes 2164736 | tf_op jit(solution)/shard_map/dot_general | solution.py:104
  93.9 2.7 %divide_convert_fusion = bf16[1,14336]{1,0:T(2,128)(2,1)S(1)} fusion(f32[1,14336]{1,0:T(1,128)S(1)} %get-tuple-element.11, f32[1,14336]{1,0:T(1,128)S(1)} %get-tuple-element.9, f32[1,14336]{1,0:T(1,128)S(1)} %get-tuple-element.7, f32[4,32768]{1,0:T(4,128)S(1)} %bitcast.211, f32[]{:T(128)} %bitcast.78, f32[]{:T(128)} %bitcast.77, f32[]{:T(128)} %bitcast.76, ...), kind=kLoop, calls=%fused_computation.69 | loop fusion | flops 114688 | bytes 258064 | tf_op jit(solution)/shard_map/convert.3
  96.6 2.5 %fusion.79 = (bf16[1,1024]{1,0:T(2,128)(2,1)S(1)}, f32[1,1024]{1,0:T(1,128)S(1)}, bf16[1,1024]{1,0:T(2,128)(2,1)S(1)}, f32[1,1024]{1,0:T(1,128)S(1)}) fusion(f32[]{:T(128)} %bitcast.47, f32[1,1024]{1,0:T(1,128)S(1)} %get-tuple-element.19, f32[]{:T(128)} %bitcast.46, f32[4,32768]{1,0:T(4,128)S(1)} %bitcast.212, f32[]{:T(128)} %bitcast.35, ...), kind=kLoop, calls=%fused_computation.164 | loop fusion | flops 8192 | bytes 28688 | tf_op jit(solution)/shard_map/convert.9
  99.1 3.8 %fusion.81 = (bf16[1,1024]{1,0:T(2,128)(2,1)S(1)}, f32[1,1024]{1,0:T(1,128)S(1)}, bf16[1,1024]{1,0:T(2,128)(2,1)S(1)}, f32[1,1024]{1,0:T(1,128)S(1)}) fusion(f32[]{:T(128)} %bitcast.50, f32[1,1024]{1,0:T(1,128)S(1)} %get-tuple-element.21, f32[]{:T(128)} %bitcast.49, f32[1,1024]{1,0:T(1,128)S(1)} %get-tuple-element.19, f32[]{:T(128)} %bitcast.48, ...), kind=kLoop, calls=%fused_computation.165 | loop fusion | flops 12288 | bytes 36888 | tf_op jit(solution)/shard_map/convert.10
  102.8 4.9 %divide_convert_fusion.3 = (bf16[1,1024]{1,0:T(2,128)(2,1)S(1)}, bf16[1,1024]{1,0:T(2,128)(2,1)S(1)}) fusion(f32[1,1024]{1,0:T(1,128)S(1)} %get-tuple-element.23, f32[1,1024]{1,0:T(1,128)S(1)} %get-tuple-element.21, f32[1,1024]{1,0:T(1,128)S(1)} %get-tuple-element.19, f32[4,32768]{1,0:T(4,128)S(1)} %bitcast.214, f32[]{:T(128)} %bitcast.54, f32[]{:T(128)} %bitcast.53, ...), kind=kLoop, calls=%fused_computation.110 | loop fusion | flops 16384 | bytes 36896 | tf_op jit(solution)/shard_map/convert.11
  107.8 1.1 fusion.25
  108.9 1.1 fusion.24
  110.0 2.0 %fusion.19 = f32[5,4,128]{2,1,0:T(4,128)S(1)} fusion(f32[5,4,128]{2,1,0:T(4,128)S(1)} %fusion.24, bf16[1,32768,128]{2,1,0:T(8,128)(2,1)} %copy-done, bf16[1,8192]{1,0:T(2,128)(2,1)S(1)} %get-tuple-element.38, bf16[1,8192]{1,0:T(2,128)(2,1)S(1)} %get-tuple-element.16, bf16[1,8192]{1,0:T(2,128)(2,1)S(1)} %get-tuple-element.14, ...), kind=kOutput, calls=%fused_computation.33 | convolution fusion | flops 8650752 | bytes 2230272 | tf_op jit(solution)/shard_map/dot_general | solution.py:104
  112.0 2.8 %fusion.23 = f32[5,4,128]{2,1,0:T(4,128)S(1)} fusion(f32[5,4,128]{2,1,0:T(4,128)S(1)} %fusion.19, bf16[1,32768,128]{2,1,0:T(8,128)(2,1)} %copy-done, bf16[1,14336]{1,0:T(2,128)(2,1)S(1)} %divide_convert_fusion, bf16[1,14336]{1,0:T(2,128)(2,1)S(1)} %get-tuple-element.10, bf16[1,14336]{1,0:T(2,128)(2,1)S(1)} %get-tuple-element.8, ...), kind=kOutput, calls=%fused_computation.37 | convolution fusion | flops 15138816 | bytes 3901440 | tf_op jit(solution)/shard_map/dot_general | solution.py:104
  114.8 5.3 %all_to_all.22 = f32[2,5,4,128]{3,2,1,0:T(4,128)S(1)} all-to-all(f32[2,5,4,128]{3,2,1,0:T(4,128)S(1)} %broadcast_in_dim.10), channel_id=1, replica_groups=mesh['grp'=2,'dp'=64] {'grp'}, dimensions={0} | all-to-all | bytes 40960 | tf_op jit(solution)/shard_map/all_to_all | solution.py:27
  120.1 0.6 fusion.67
  120.7 2.6 %fusion.6 = bf16[32768,128]{1,0:T(8,128)(2,1)S(1)} fusion(bf16[1,32768,128]{2,1,0:T(8,128)(2,1)} %copy-done, bf16[5,4,128]{2,1,0:T(4,128)(2,1)S(1)} %get-tuple-element.4, bf16[1,8192]{1,0:T(2,128)(2,1)S(1)} %get-tuple-element.39, bf16[1,8192]{1,0:T(2,128)(2,1)S(1)} %get-tuple-element.40, bf16[1,8192]{1,0:T(2,128)(2,1)S(1)} %get-tuple-element.42, ...), kind=kOutput, calls=%fused_computation.11 | convolution fusion | flops 11796479 | bytes 4326400 | tf_op jit(solution)/shard_map/dot_general | solution.py:115
  123.3 1.3 fusion.15
  124.6 1.3 fusion.14
  125.9 3.0 %fusion.5 = bf16[32768,128]{1,0:T(8,128)(2,1)S(1)} fusion(bf16[32768,128]{1,0:T(8,128)(2,1)S(1)} %fusion.14, bf16[1,32768,128]{2,1,0:T(8,128)(2,1)} %copy-done, bf16[5,4,128]{2,1,0:T(4,128)(2,1)S(1)} %get-tuple-element.4, bf16[1,8192]{1,0:T(2,128)(2,1)S(1)} %get-tuple-element.38, bf16[1,8192]{1,0:T(2,128)(2,1)S(1)} %get-tuple-element.16, ...), kind=kOutput, calls=%fused_computation.10 | convolution fusion | flops 11796480 | bytes 4326400 | tf_op jit(solution)/shard_map/dot_general | solution.py:115
  128.9 4.4 %fusion.1 = bf16[32768,128]{1,0:T(8,128)(2,1)S(1)} fusion(bf16[32768,128]{1,0:T(8,128)(2,1)S(1)} %fusion.5, bf16[1,32768,128]{2,1,0:T(8,128)(2,1)} %copy-done, bf16[5,4,128]{2,1,0:T(4,128)(2,1)S(1)} %get-tuple-element.4, bf16[1,14336]{1,0:T(2,128)(2,1)S(1)} %divide_convert_fusion, bf16[1,14336]{1,0:T(2,128)(2,1)S(1)} %get-tuple-element.10, ...), kind=kOutput, calls=%fused_computation.2 | convolution fusion | flops 20643840 | bytes 7570432 | tf_op jit(solution)/shard_map/dot_general | solution.py:115
  133.3 1.0 fusion.31
  134.3 2.4 %copy-done.3 = bf16[32768,128]{1,0:T(8,128)(2,1)} copy-done((bf16[32768,128]{1,0:T(8,128)(2,1)}, bf16[32768,128]{1,0:T(8,128)(2,1)S(1)}, u32[]{:S(2)}) %copy-start.3) | copy-done | bytes 8388632
  (30 shorter events, 0.9 us)
Async XLA Ops:
  8.4 3.4 %copy-start = (bf16[1,32768,128]{2,1,0:T(8,128)(2,1)}, bf16[1,32768,128]{2,1,0:T(8,128)(2,1)S(1)}, u32[]{:S(2)}) copy-start(bf16[1,32768,128]{2,1,0:T(8,128)(2,1)S(1)} %add_convert_fusion) | copy-start | bytes 25165828
  8.4 39.5 %copy-start.2 = (s32[5]{0:T(128)S(1)}, s32[5]{0:T(128)}, u32[]{:S(2)}) copy-start(s32[5]{0:T(128)} %param.8) | copy-start | bytes 64
  43.2 17.0 %all-to-all-start.2 = ((f32[64,4,512]{2,1,0:T(4,128)}), f32[64,4,512]{2,1,0:T(4,128)S(1)}, u32[]{:S(2)}, u32[]{:S(2)}) async-start(f32[64,4,512]{2,1,0:T(4,128)} %broadcast_in_dim.9), calls=%async_computation.2 | async-start | bytes 1048576 | tf_op jit(solution)/shard_map/all_to_all | solution.py:27
  123.3 10.0 %copy-start.1 = (pred[14336]{0:T(1024)(128)(4,1)S(1)}, pred[14336]{0:T(1024)(128)(4,1)}, u32[]{:S(2)}) copy-start(pred[14336]{0:T(1024)(128)(4,1)} %constant.43.clone.1) | copy-start | bytes 43012
  133.3 3.5 %copy-start.3 = (bf16[32768,128]{1,0:T(8,128)(2,1)}, bf16[32768,128]{1,0:T(8,128)(2,1)S(1)}, u32[]{:S(2)}) copy-start(bf16[32768,128]{1,0:T(8,128)(2,1)S(1)} %fusion.1) | copy-start | bytes 25165828
where the time goes:
time: 138 us; the launch traced here: 137 us
  other arithmetic  50.2 us (36%)
  blocking collectives  34.6 us (25%)
  matrix products  25.1 us (18%)
  local copies, waits for them, and re-layouts  9.55 us (7%)
  waiting for transfers between devices  8.48 us (6%)
  starting transfers between devices  4.63 us (3%)
  between operations  4.15 us (3%)
    another operation x12, other arithmetic  32.3 us
    all_to_all x1, blocking collectives, sent_and_summed(): lax.all_to_all(tiles, axis, split_axis=0, concat_axis=0, tiled=True)  23.7 us
    dot_general x5, matrix products, body(): lax.dot_general(bases[layer_id], q_round[layer_id], (((0,), (0,)), ((), (...  12.5 us
    all_to_all x2, blocking collectives, sent_to_all(): lax.all_to_all(jnp.broadcast_to(x[None], (count, *x.shape)), axis, 0, 0,...  10.9 us
    dot_general x5, matrix products, body(): jnp.dot(bases[layer_id], compensated[start_row:start_row + count], prefer...  9.06 us
    all_to_all x1, waiting for transfers between devices, sent_to_all(): lax.all_to_all(jnp.broadcast_to(x[None], (count, *x.shape)), axis, 0, 0,...  8.48 us
    convert_element_type x1, other arithmetic, body(): (grad[0].astype(jnp.float32) + residual[0].astype(jnp.float32)).astype(jn...  7.01 us
    another operation x15, other arithmetic, orthonormal(): return whiten(jnp.linalg.cholesky(gram_matrix), projected)  5.17 us
  transfers between devices with their start and end apart: 1, of which 1 were waited for; matrix products, arithmetic and copies ran while one was open for 0% of the time, Pallas kernels for 0%

commit v1 on v0

v1 whole, which is shorter than its diff:
```python
import functools

import jax
import jax.numpy as jnp
from jax import lax
from jax.experimental import pallas as pl
from jax.experimental.pallas import tpu as pltpu
from jax.sharding import PartitionSpec as P

D = 8192
KV = 1024
FF_WIN = 14336
SIZES = (D, KV, KV, D, FF_WIN)
ROWS = sum(SIZES)
LANES = 128
TILE = 512
HALF = TILE // 2
TILES = ROWS // TILE
GROUP = 8
EPSILON = 1e-06
SWAP = ((0, 1), (1, 0))
F32, BF16 = jnp.float32, jnp.bfloat16
MIB = 1 << 20


def tile_layers():
    return [layer for layer, rows in enumerate(SIZES) for _ in range(rows // TILE)]


def layer_starts():
    starts, at = [], 0
    for rows in SIZES:
        starts.append(at)
        at += rows // TILE
    return starts


VM = pl.BlockSpec(memory_space=pltpu.VMEM)
SM = pl.BlockSpec(memory_space=pltpu.SMEM)
HB = pl.BlockSpec(memory_space=pl.ANY)


CHUNK_TILES = 4
CHUNK = CHUNK_TILES * TILE
CHUNKS = ROWS // CHUNK


def project_kernel(g_ref, grad, residual, q_ref, comp_ref, keep_ref, send_ref, gbuf, rbuf, lhs, sems):
    def copies(c):
        rows = pl.ds(c * CHUNK, CHUNK)
        return (
            pltpu.make_async_copy(grad.at[0, rows], gbuf.at[rows], sems.at[0, c]),
            pltpu.make_async_copy(residual.at[0, rows], rbuf.at[rows], sems.at[1, c]),
        )

    for c in range(CHUNKS):
        for copy in copies(c):
            copy.start()
    own = g_ref[0]
    for layer in range(len(SIZES)):
        q = q_ref[layer].astype(BF16).astype(F32)
        zero = jnp.zeros_like(q)
        straight = jnp.concatenate(
            [jnp.concatenate([q, zero], 1), jnp.concatenate([zero, q], 1)], 0
        )
        crossed = jnp.concatenate(
            [jnp.concatenate([zero, q], 1), jnp.concatenate([q, zero], 1)], 0
        )
        lhs[layer] = jnp.where(own == 0, straight, crossed)

    def chunk(c, layers):
        for copy in copies(c):
            copy.wait()
        for k in range(CHUNK_TILES):
            t = c * CHUNK_TILES + k
            halves = []
            for h in range(2):
                rows = pl.ds(pl.multiple_of(t * TILE + h * HALF, HALF), HALF)
                value = (gbuf[rows].astype(F32) + rbuf[rows].astype(F32)).astype(BF16)
                comp_ref[rows] = value
                halves.append(value)
            out = lax.dot_general(
                lhs[layers[k]].astype(BF16),
                jnp.concatenate(halves, 1),
                (((1,), (1,)), ((), ())),
                preferred_element_type=F32,
            )
            keep_ref[t] = out[:4]
            send_ref[t] = out[4:]

    layers = tile_layers()
    groups = [tuple(layers[c * CHUNK_TILES : (c + 1) * CHUNK_TILES]) for c in range(CHUNKS)]
    c = 0
    while c < CHUNKS:
        end = c
        while end < CHUNKS and groups[end] == groups[c]:
            end += 1
        if end - c == 1:
            chunk(c, groups[c])
        else:
            lax.fori_loop(c, end, lambda i, _, now=groups[c]: chunk(i, now), None)
        c = end


def project(own, grad, residual, q_prev):
    share = jax.ShapeDtypeStruct((TILES, 4, HALF), F32)
    return pl.pallas_call(
        project_kernel,
        out_shape=(pltpu.VMEM((ROWS, LANES), BF16), share, share),
        in_specs=[SM, HB, HB, VM],
        out_specs=(VM, VM, VM),
        scratch_shapes=[
            pltpu.VMEM((ROWS, LANES), BF16),
            pltpu.VMEM((ROWS, LANES), BF16),
            pltpu.VMEM((len(SIZES), 8, 2 * LANES), F32),
            pltpu.SemaphoreType.DMA((2, CHUNKS)),
        ],
        compiler_params=pltpu.CompilerParams(vmem_limit_bytes=30 * MIB),
        name="project",
    )(own, grad, residual, q_prev)


def spread_kernel(x_ref, o_ref):
    total = x_ref[0]
    for i in range(1, TILES):
        total = total + x_ref[i]
    total = total * 0.5
    for i in range(TILES):
        o_ref[i] = total


def spread(x):
    return pl.pallas_call(
        spread_kernel,
        out_shape=jax.ShapeDtypeStruct((TILES, 4, HALF), F32),
        in_specs=[VM],
        out_specs=VM,
        compiler_params=pltpu.CompilerParams(vmem_limit_bytes=2 * MIB),
        name="spread",
    )(x)


def lane_sum(x):
    return jnp.sum(x, axis=1, keepdims=True)


def coefficients(grams):
    lane = lax.broadcasted_iota(jnp.int32, (8, LANES), 1)
    row = lax.broadcasted_iota(jnp.int32, (8, LANES), 0) % 4
    entry = {}
    for k in range(4):
        packed = jnp.zeros((8, LANES), F32)
        for layer, sums in enumerate(grams):
            s = sums[k][:, :LANES] + sums[k][:, LANES:]
            s = s + pltpu.roll(s, 4, 0)
            packed = jnp.where(lane == layer, lane_sum(s), packed)
        for i in range(k, 4):
            value = jnp.broadcast_to(packed[i : i + 1], (8, LANES))
            entry[i, i - k] = value + EPSILON if k == 0 else value
    g = entry
    i0 = lax.rsqrt(g[0, 0])
    l10, l20, l30 = g[1, 0] * i0, g[2, 0] * i0, g[3, 0] * i0
    i1 = lax.rsqrt(g[1, 1] - l10 * l10)
    l21 = (g[2, 1] - l20 * l10) * i1
    l31 = (g[3, 1] - l30 * l10) * i1
    i2 = lax.rsqrt(g[2, 2] - l20 * l20 - l21 * l21)
    l32 = (g[3, 2] - l30 * l20 - l31 * l21) * i2
    i3 = lax.rsqrt(g[3, 3] - l30 * l30 - l31 * l31 - l32 * l32)
    x = {(0, 0): i0, (1, 1): i1, (2, 2): i2, (3, 3): i3}
    x[1, 0] = -(l10 * i0) * i1
    x[2, 1] = -(l21 * i1) * i2
    x[3, 2] = -(l32 * i2) * i3
    x[2, 0] = -(l20 * i0 + l21 * x[1, 0]) * i2
    x[3, 1] = -(l31 * i1 + l32 * x[2, 1]) * i3
    x[3, 0] = -(l30 * i0 + l31 * x[1, 0] + l32 * x[2, 0]) * i3
    columns = []
    for k in range(4):
        packed = jnp.zeros((8, LANES), F32)
        for i in range(k, 4):
            packed = jnp.where(row == i, x[i, i - k], packed)
        columns.append(
            [
                jnp.broadcast_to(packed[:, layer : layer + 1], (8, 2 * LANES))
                for layer in range(len(SIZES))
            ]
        )
    return columns


def basis_kernel(g_ref, mine, other, comp, owned_hbm, q_ref, turned_ref, joined, stacked, owned, sem):
    own, place = g_ref[0], g_ref[1]
    counts = [rows // TILE for rows in SIZES]
    starts = layer_starts()

    owned[...] = jnp.zeros_like(owned)
    for layer, count in enumerate(counts):

        @pl.when(g_ref[2 + layer] == place)
        def _():
            def step(k, _):
                at = pl.multiple_of(k * TILE + own * HALF, HALF)
                owned[0, :, pl.ds(at, HALF)] = mine[starts[layer] + k]
                at = pl.multiple_of(k * TILE + (1 - own) * HALF, HALF)
                owned[0, :, pl.ds(at, HALF)] = other[starts[layer] + k]

            lax.fori_loop(0, count, step, None)

    copy = pltpu.make_async_copy(owned, owned_hbm, sem)
    copy.start()

    grams = []
    for layer, count in enumerate(counts):
        sums = [None] * 4
        for t in range(starts[layer], starts[layer] + count):
            v = jnp.concatenate([mine[t], other[t]], 0)
            joined[t] = v
            for k in range(4):
                term = v * (pltpu.roll(v, k, 0) if k else v)
                sums[k] = term if sums[k] is None else sums[k] + term
        grams.append(sums)
    columns = coefficients(grams)

    for layer, count in enumerate(counts):
        total = None
        for t in range(starts[layer], starts[layer] + count):
            v = joined[t]
            basis = v * columns[0][layer]
            for k in range(1, 4):
                basis = basis + pltpu.roll(v, k, 0) * columns[k][layer]
            rounded = basis.astype(BF16)
            back = rounded.astype(F32)
            at = (t % GROUP) * 16
            stacked[t // GROUP, at : at + 8] = back[:, :LANES]
            stacked[t // GROUP, at + 8 : at + 16] = back[:, LANES:]
            first = comp[pl.ds(pl.multiple_of(t * TILE + own * HALF, HALF), HALF)]
            second = comp[pl.ds(pl.multiple_of(t * TILE + (1 - own) * HALF, HALF), HALF)]
            part = jnp.dot(
                rounded, jnp.concatenate([first, second], 1), preferred_element_type=F32
            )
            total = part if total is None else total + part
        q_ref[layer] = total[:4, :LANES] + total[4:, LANES:]
    for n in range(TILES // GROUP):
        turned_ref[n] = stacked[n].T.astype(BF16)
    copy.wait()


def orthonormal_bases(scalars, mine, other, comp):
    return pl.pallas_call(
        basis_kernel,
        out_shape=(
            jax.ShapeDtypeStruct((1, 4, max(SIZES)), F32),
            jax.ShapeDtypeStruct((len(SIZES), 4, LANES), F32),
            pltpu.VMEM((TILES // GROUP, LANES, LANES), BF16),
        ),
        in_specs=[SM, VM, VM, VM],
        out_specs=(HB, VM, VM),
        scratch_shapes=[
            pltpu.VMEM((TILES, 8, HALF), F32),
            pltpu.VMEM((TILES // GROUP, LANES, LANES), F32),
            pltpu.VMEM((1, 4, max(SIZES)), F32),
            pltpu.SemaphoreType.DMA,
        ],
        compiler_params=pltpu.CompilerParams(vmem_limit_bytes=16 * MIB),
        name="bases",
    )(scalars, mine, other, comp)


def residual_kernel(g_ref, q_mine, q_other, turned, comp, out_hbm, q_ref, weights, obuf, sems):
    own = g_ref[0]
    layers = tile_layers()
    q_new = (q_mine[...] + q_other[...]) * 0.5
    q_ref[...] = q_new
    rounded = q_new.astype(BF16).astype(F32)
    weights[...] = jnp.zeros_like(weights)
    groups = TILES // GROUP
    for n in range(groups):
        for c in range(2 * GROUP):
            q = rounded[layers[n * GROUP + c // 2]]
            h = c % 2
            weights[n, c * 8 : c * 8 + 8, h * LANES : (h + 1) * LANES] = jnp.concatenate([q, q], 0)
    lane = lax.broadcasted_iota(jnp.int32, (LANES, LANES), 1)

    def copy(n):
        rows = pl.ds(n * GROUP * TILE, GROUP * TILE)
        return pltpu.make_async_copy(obuf.at[rows], out_hbm.at[0, rows], sems.at[n])

    def group(n, _):
        w = weights[n].astype(BF16)
        left = turned[n]
        for k in range(GROUP):
            for other in range(2):
                chosen = (lane // 16 == k) & ((lane // 4) % 2 == other)
                update = jnp.dot(
                    jnp.where(chosen, left, jnp.zeros_like(left)), w, preferred_element_type=F32
                )
                which = own if other == 0 else 1 - own
                at = pl.multiple_of((n * GROUP + k) * TILE + which * HALF, HALF)
                for h in range(2):
                    rows = pl.ds(pl.multiple_of(at + h * LANES, LANES), LANES)
                    obuf[rows] = (
                        comp[rows].astype(F32) - update[:, h * LANES : (h + 1) * LANES]
                    ).astype(BF16)
        copy(n).start()

    lax.fori_loop(0, groups, group, None)
    for n in range(groups):
        copy(n).wait()


def new_residual(scalars, q_mine, q_other, turned, comp):
    return pl.pallas_call(
        residual_kernel,
        out_shape=(
            jax.ShapeDtypeStruct((1, ROWS, LANES), BF16),
            jax.ShapeDtypeStruct((len(SIZES), 4, LANES), F32),
        ),
        in_specs=[SM, VM, VM, VM, VM],
        out_specs=(HB, VM),
        scratch_shapes=[
            pltpu.VMEM((TILES // GROUP, LANES, 2 * LANES), F32),
            pltpu.VMEM((ROWS, LANES), BF16),
            pltpu.SemaphoreType.DMA((TILES // GROUP,)),
        ],
        compiler_params=pltpu.CompilerParams(vmem_limit_bytes=24 * MIB),
        name="new_residual",
    )(scalars, q_mine, q_other, turned, comp)


def body(grad, residual, q_prev, owner_table):
    own = lax.axis_index("grp").astype(jnp.int32)
    place = lax.axis_index("dp").astype(jnp.int32)
    scalars = jnp.concatenate([jnp.stack([own, place]), owner_table])
    comp, keep, send = project(scalars, grad, residual, q_prev)
    both = keep + lax.ppermute(send, "grp", SWAP)
    arrived = lax.all_to_all(both, "dp", 0, 0, tiled=True)
    mine = lax.all_to_all(spread(arrived), "dp", 0, 0, tiled=True)
    other = lax.ppermute(mine, "grp", SWAP)
    owned, q_part, turned = orthonormal_bases(scalars, mine, other, comp)
    q_there = lax.ppermute(q_part, "grp", SWAP)
    out, q_new = new_residual(scalars, q_part, q_there, turned, comp)
    return out, q_new, owned


def solution(mesh):
    in_specs = (P("grp", None, "dp"), P("grp", None, "dp"), P(None, None, "dp"), P())
    out_specs = (P("grp", None, "dp"), P(None, None, "dp"), P("dp", None, None))
    return jax.shard_map(body, mesh=mesh, in_specs=in_specs, out_specs=out_specs, check_vma=False)
```

time: 138 us -> 64.1 us (0.46)
  other arithmetic: 50.2 us -> 0.8 us
  matrix products: 25.1 us -> 0 us
  Pallas kernels: 0 us -> 15.3 us
  local copies, waits for them, and re-layouts: 9.55 us -> 4.08 us
  waiting for transfers between devices: 8.48 us -> 3.16 us
  between operations: 4.15 us -> 0.66 us
    another operation x27 -> x0, other arithmetic: 37.4 us -> none
    dot_general x20 -> x0, matrix products: 25.1 us -> none  [the longest x5 12.5 us: body(): lax.dot_general(bases[layer_id], q_round[layer_id], (((0,), (0,)), ((), (...]
    pallas_call x0 -> x4, Pallas kernels: none -> 15.3 us  [the longest x1 6.71 us: project(): pl.pallas_call(project_kernel, out_shape=(pltpu.VMEM((ROWS, LANES), BF16)...]
    all_to_all x1 -> x0, waiting for transfers between devices: 8.48 us -> none  [sent_to_all(): lax.all_to_all(jnp.broadcast_to(x[None], (count, *x.shape)), axis, 0, 0,...]
    convert_element_type x3 -> x0, other arithmetic: 8.33 us -> none  [the longest x1 7.01 us: body(): (grad[0].astype(jnp.float32) + residual[0].astype(jnp.float32)).astype(jn...]
    ppermute x0 -> x3, starting transfers between devices: none -> 4.97 us  [the longest x1 3.06 us: body(): other = lax.ppermute(mine, 'grp', SWAP)]
    all_to_all x1 -> x0, starting transfers between devices: 4.63 us -> none  [sent_to_all(): lax.all_to_all(jnp.broadcast_to(x[None], (count, *x.shape)), axis, 0, 0,...]
    slice x8 -> x0, local copies, waits for them, and re-layouts: 4.09 us -> none  [the longest x5 3.41 us: whiten(): running = running - lower_factor[..., i, k, None] * solved[k]]
  transfers between devices with their start and end apart: 1 -> 3, of which waited for: 1 -> 3; matrix products, arithmetic and copies ran while one was open for 0% -> 0% of each run, Pallas kernels for 0% -> 0%
where the time goes in v1:
time: 64.1 us; the launch traced here: 63.8 us
  blocking collectives  34.8 us (54%)
  Pallas kernels  15.3 us (24%)
  starting transfers between devices  4.97 us (8%)
  local copies, waits for them, and re-layouts  4.08 us (6%)
  waiting for transfers between devices  3.16 us (5%)
  other arithmetic  0.8 us (1%)
  between operations  0.66 us (1%)
    all_to_all x1, blocking collectives, body(): arrived = lax.all_to_all(both, 'dp', 0, 0, tiled=True)  21 us
    all_to_all x1, blocking collectives, body(): mine = lax.all_to_all(spread(arrived), 'dp', 0, 0, tiled=True)  13.8 us
    pallas_call x1, Pallas kernels, project(): pl.pallas_call(project_kernel, out_shape=(pltpu.VMEM((ROWS, LANES), BF16)...  6.71 us
    pallas_call x1, Pallas kernels, new_residual(): pl.pallas_call(residual_kernel, out_shape=(jax.ShapeDtypeStruct((1, ROWS,...  5.82 us
    unnamed x4, local copies, waits for them, and re-layouts  4.08 us
    ppermute x1, starting transfers between devices, body(): other = lax.ppermute(mine, 'grp', SWAP)  3.06 us
    pallas_call x1, Pallas kernels, orthonormal_bases(): pl.pallas_call(basis_kernel, out_shape=(jax.ShapeDtypeStruct((1, 4, max(S...  2.72 us
    ppermute x1, starting transfers between devices, body(): both = keep + lax.ppermute(send, 'grp', SWAP)  1.46 us
  transfers between devices with their start and end apart: 3, of which 3 were waited for; matrix products, arithmetic and copies ran while one was open for 0% of the time, Pallas kernels for 0%

profile of v1, /device:TPU:1, one launch (start us, length us, event | category | flops | bytes accessed | tf_op | source)
XLA Modules:
  0.0 63.8 jit_solution(18264675674441109214)
XLA Ops:
  0.6 0.7 %pad_add_fusion.g_ref = s32[7]{0:T(128)S(1)} fusion(s32[5]{0:T(128)} %param.7, s32[1]{0:T(128)} %bitcast.1, s32[1]{0:T(128)} %bitcast), kind=kLoop, calls=%fused_computation | loop fusion | flops 14 | bytes 56 | tf_op jit(solution)/shard_map/concatenate | solution.py:332
  1.4 0.0 copy-start
  1.4 3.4 %copy-done = bf16[1,32768,128]{2,1,0:T(8,128)(2,1)S(1)} copy-done((bf16[1,32768,128]{2,1,0:T(8,128)(2,1)S(1)}, bf16[1,32768,128]{2,1,0:T(8,128)(2,1)}, u32[]{:S(2)}) %copy-start) | copy-done | bytes 8388632
  4.8 0.0 copy-start.1
  4.8 0.7 %copy-done.1 = f32[5,4,128]{2,1,0:T(4,128)S(1)} copy-done((f32[5,4,128]{2,1,0:T(4,128)S(1)}, f32[5,4,128]{2,1,0:T(4,128)}, u32[]{:S(2)}) %copy-start.1) | copy-done | bytes 10264
  5.5 6.7 %project.1 = (bf16[32768,128]{1,0:T(8,128)(2,1)S(1)}, f32[64,4,256]{2,1,0:T(4,128)S(1)}, f32[64,4,256]{2,1,0:T(4,128)S(1)}) custom-call(s32[7]{0:T(128)S(1)} %pad_add_fusion.g_ref, bf16[1,32768,128]{2,1,0:T(8,128)(2,1)S(1)} %copy-done, bf16[1,32768,128]{2,1,0:T(8,128)(2,1)} %residual.1, f32[5,4,128]{2,1,0:T(4,128)S(1)} %copy-done.1), custom_call_target="tpu_custom_call" | custom-call | tf_op jit(solution)/shard_map/project/pallas_call | solution.py:107
  12.2 1.5 %collective-permute-start = (f32[64,4,256]{2,1,0:T(4,128)S(1)}, f32[64,4,256]{2,1,0:T(4,128)S(1)}, u32[]{:S(2)}, u32[]{:S(2)}) collective-permute-start(f32[64,4,256]{2,1,0:T(4,128)S(1)} %get-tuple-element.12), channel_id=1, source_target_pairs={{0,64},{64,0},{1,65},{65,1},{2,66},{66,2},{3,67},{67,3},{4,68},{68... | collective-permute-start | bytes 786440 | tf_op jit(solution)/shard_map/ppermute | solution.py:334
  13.6 1.2 %collective-permute-done = f32[64,4,256]{2,1,0:T(4,128)S(1)} collective-permute-done((f32[64,4,256]{2,1,0:T(4,128)S(1)}, f32[64,4,256]{2,1,0:T(4,128)S(1)}, u32[]{:S(2)}, u32[]{:S(2)}) %collective-permute-start) | collective-permute-done | bytes 262176 | tf_op jit(solution)/shard_map/ppermute | solution.py:334
  14.8 0.1 add.3
  14.9 21.0 %all_to_all.10.x_ref = f32[64,4,256]{2,1,0:T(4,128)S(1)} all-to-all(f32[64,4,256]{2,1,0:T(4,128)S(1)} %add.3), channel_id=1, replica_groups=mesh['grp'=2,'dp'=64] {'dp'}, dimensions={0} | all-to-all | bytes 524288 | tf_op jit(solution)/shard_map/all_to_all | solution.py:335
  35.8 0.1 spread.1
  35.9 13.8 %all_to_all.11.mine = f32[64,4,256]{2,1,0:T(4,128)S(1)} all-to-all(f32[64,4,256]{2,1,0:T(4,128)S(1)} %spread.1), channel_id=1, replica_groups=mesh['grp'=2,'dp'=64] {'dp'}, dimensions={0} | all-to-all | bytes 524288 | tf_op jit(solution)/shard_map/all_to_all | solution.py:336
  49.7 3.1 %collective-permute-start.1 = (f32[64,4,256]{2,1,0:T(4,128)S(1)}, f32[64,4,256]{2,1,0:T(4,128)S(1)}, u32[]{:S(2)}, u32[]{:S(2)}) collective-permute-start(f32[64,4,256]{2,1,0:T(4,128)S(1)} %all_to_all.11.mine), channel_id=1, source_target_pairs={{0,64},{64,0},{1,65},{65,1},{2,66},{66,2},{3,67},{67,3},{4,68},{68... | collective-permute-start | bytes 786440 | tf_op jit(solution)/shard_map/ppermute | solution.py:337
  52.8 1.2 %collective-permute-done.1.other = f32[64,4,256]{2,1,0:T(4,128)S(1)} collective-permute-done((f32[64,4,256]{2,1,0:T(4,128)S(1)}, f32[64,4,256]{2,1,0:T(4,128)S(1)}, u32[]{:S(2)}, u32[]{:S(2)}) %collective-permute-start.1) | collective-permute-done | bytes 262176 | tf_op jit(solution)/shard_map/ppermute | solution.py:337
  53.9 2.7 %bases.1 = (f32[1,4,14336]{2,1,0:T(4,128)}, f32[5,4,128]{2,1,0:T(4,128)S(1)}, bf16[8,128,128]{2,1,0:T(8,128)(2,1)S(1)}) custom-call(s32[7]{0:T(128)S(1)} %pad_add_fusion.g_ref, f32[64,4,256]{2,1,0:T(4,128)S(1)} %all_to_all.11.mine, f32[64,4,256]{2,1,0:T(4,128)S(1)} %collective-permute-done.1.other, bf16[32768,128]{1,0:T(8,128)(2,1)S(1)} %get-tuple-element.13.comp), custom_call_target="tpu_custom_call" | custom-call | tf_op jit(solution)/shard_map/bases/pallas_call | solution.py:248
  56.7 0.5 collective-permute-start.2
  57.1 0.8 %collective-permute-done.2.q_other = f32[5,4,128]{2,1,0:T(4,128)S(1)} collective-permute-done((f32[5,4,128]{2,1,0:T(4,128)S(1)}, f32[5,4,128]{2,1,0:T(4,128)S(1)}, u32[]{:S(2)}, u32[]{:S(2)}) %collective-permute-start.2) | collective-permute-done | bytes 10272 | tf_op jit(solution)/shard_map/ppermute | solution.py:339
  58.0 5.8 %new_residual.1 = (bf16[1,32768,128]{2,1,0:T(8,128)(2,1)}, f32[5,4,128]{2,1,0:T(4,128)}) custom-call(s32[7]{0:T(128)S(1)} %pad_add_fusion.g_ref, f32[5,4,128]{2,1,0:T(4,128)S(1)} %get-tuple-element.14.q_mine, f32[5,4,128]{2,1,0:T(4,128)S(1)} %collective-permute-done.2.q_other, bf16[8,128,128]{2,1,0:T(8,128)(2,1)S(1)} %get-tuple-element.15.turned, ...), custom_call_target="tpu_custom_call" | custom-call | tf_op jit(solution)/shard_map/new_residual/pallas_call | solution.py:311
Async XLA Ops:
  1.4 3.4 %copy-start = (bf16[1,32768,128]{2,1,0:T(8,128)(2,1)S(1)}, bf16[1,32768,128]{2,1,0:T(8,128)(2,1)}, u32[]{:S(2)}) copy-start(bf16[1,32768,128]{2,1,0:T(8,128)(2,1)} %grad.1) | copy-start | bytes 25165828
  4.8 0.7 %copy-start.1 = (f32[5,4,128]{2,1,0:T(4,128)S(1)}, f32[5,4,128]{2,1,0:T(4,128)}, u32[]{:S(2)}) copy-start(f32[5,4,128]{2,1,0:T(4,128)} %q_ref.1) | copy-start | bytes 30724
  12.2 2.6 %collective-permute-start = (f32[64,4,256]{2,1,0:T(4,128)S(1)}, f32[64,4,256]{2,1,0:T(4,128)S(1)}, u32[]{:S(2)}, u32[]{:S(2)}) collective-permute-start(f32[64,4,256]{2,1,0:T(4,128)S(1)} %get-tuple-element.12), channel_id=1, source_target_pairs={{0,64},{64,0},{1,65},{65,1},{2,66},{66,2},{3,67},{67,3},{4,68},{68... | collective-permute-start | bytes 786440 | tf_op jit(solution)/shard_map/ppermute | solution.py:334
  49.7 4.2 %collective-permute-start.1 = (f32[64,4,256]{2,1,0:T(4,128)S(1)}, f32[64,4,256]{2,1,0:T(4,128)S(1)}, u32[]{:S(2)}, u32[]{:S(2)}) collective-permute-start(f32[64,4,256]{2,1,0:T(4,128)S(1)} %all_to_all.11.mine), channel_id=1, source_target_pairs={{0,64},{64,0},{1,65},{65,1},{2,66},{66,2},{3,67},{67,3},{4,68},{68... | collective-permute-start | bytes 786440 | tf_op jit(solution)/shard_map/ppermute | solution.py:337
  56.7 1.3 %collective-permute-start.2 = (f32[5,4,128]{2,1,0:T(4,128)S(1)}, f32[5,4,128]{2,1,0:T(4,128)S(1)}, u32[]{:S(2)}, u32[]{:S(2)}) collective-permute-start(f32[5,4,128]{2,1,0:T(4,128)S(1)} %get-tuple-element.14.q_mine), channel_id=1, source_target_pairs={{0,64},{64,0},{1,65},{65,1},{2,66},{66,2},{3,67},{67,3},{4,68},{68... | collective-permute-start | bytes 30728 | tf_op jit(solution)/shard_map/ppermute | solution.py:339

commit v2 on v1

--- a/solution.py
+++ b/solution.py
@@ -37,7 +37,7 @@
 
 VM = pl.BlockSpec(memory_space=pltpu.VMEM)
 SM = pl.BlockSpec(memory_space=pltpu.SMEM)
-HB = pl.BlockSpec(memory_space=pl.ANY)
+HB = pl.BlockSpec(memory_space=pltpu.HBM)
 
 
 CHUNK_TILES = 4
@@ -45,7 +45,7 @@
 CHUNKS = ROWS // CHUNK
 
 
-def project_kernel(g_ref, grad, residual, q_ref, comp_ref, keep_ref, send_ref, gbuf, rbuf, lhs, sems):
+def project_kernel(grad, residual, q_hbm, comp_ref, keep_ref, send_ref, gbuf, rbuf, q_ref, lhs, sems, q_sem):
     def copies(c):
         rows = pl.ds(c * CHUNK, CHUNK)
         return (
@@ -53,10 +53,13 @@
             pltpu.make_async_copy(residual.at[0, rows], rbuf.at[rows], sems.at[1, c]),
         )
 
+    q_copy = pltpu.make_async_copy(q_hbm, q_ref, q_sem)
+    q_copy.start()
     for c in range(CHUNKS):
         for copy in copies(c):
             copy.start()
-    own = g_ref[0]
+    own = lax.axis_index("grp")
+    q_copy.wait()
     for layer in range(len(SIZES)):
         q = q_ref[layer].astype(BF16).astype(F32)
         zero = jnp.zeros_like(q)
@@ -102,22 +105,24 @@
         c = end
 
 
-def project(own, grad, residual, q_prev):
+def project(grad, residual, q_prev):
     share = jax.ShapeDtypeStruct((TILES, 4, HALF), F32)
     return pl.pallas_call(
         project_kernel,
         out_shape=(pltpu.VMEM((ROWS, LANES), BF16), share, share),
-        in_specs=[SM, HB, HB, VM],
+        in_specs=[HB, HB, HB],
         out_specs=(VM, VM, VM),
         scratch_shapes=[
             pltpu.VMEM((ROWS, LANES), BF16),
             pltpu.VMEM((ROWS, LANES), BF16),
+            pltpu.VMEM((len(SIZES), 4, LANES), F32),
             pltpu.VMEM((len(SIZES), 8, 2 * LANES), F32),
             pltpu.SemaphoreType.DMA((2, CHUNKS)),
+            pltpu.SemaphoreType.DMA,
         ],
         compiler_params=pltpu.CompilerParams(vmem_limit_bytes=30 * MIB),
         name="project",
-    )(own, grad, residual, q_prev)
+    )(*(pltpu.with_memory_space_constraint(x, pltpu.HBM) for x in (grad, residual, q_prev)))
 
 
 def spread_kernel(x_ref, o_ref):
@@ -187,15 +192,15 @@
     return columns
 
 
-def basis_kernel(g_ref, mine, other, comp, owned_hbm, q_ref, turned_ref, joined, stacked, owned, sem):
-    own, place = g_ref[0], g_ref[1]
+def basis_kernel(owner, mine, other, comp, owned_hbm, q_ref, turned_ref, joined, stacked, owned, sem):
+    own, place = lax.axis_index("grp"), lax.axis_index("dp")
     counts = [rows // TILE for rows in SIZES]
     starts = layer_starts()
 
     owned[...] = jnp.zeros_like(owned)
     for layer, count in enumerate(counts):
 
-        @pl.when(g_ref[2 + layer] == place)
+        @pl.when(owner[layer] == place)
         def _():
             def step(k, _):
                 at = pl.multiple_of(k * TILE + own * HALF, HALF)
@@ -244,7 +249,7 @@
     copy.wait()
 
 
-def orthonormal_bases(scalars, mine, other, comp):
+def orthonormal_bases(owner_table, mine, other, comp):
     return pl.pallas_call(
         basis_kernel,
         out_shape=(
@@ -262,82 +267,84 @@
         ],
         compiler_params=pltpu.CompilerParams(vmem_limit_bytes=16 * MIB),
         name="bases",
-    )(scalars, mine, other, comp)
-
-
-def residual_kernel(g_ref, q_mine, q_other, turned, comp, out_hbm, q_ref, weights, obuf, sems):
-    own = g_ref[0]
+    )(owner_table, mine, other, comp)
+
+
+PIECE = 4
+PIECES = TILES // PIECE
+
+
+def residual_kernel(q_mine, q_other, turned, comp, out_hbm, q_ref, weights, obuf, sems):
+    own = lax.axis_index("grp")
     layers = tile_layers()
     q_new = (q_mine[...] + q_other[...]) * 0.5
     q_ref[...] = q_new
     rounded = q_new.astype(BF16).astype(F32)
-    weights[...] = jnp.zeros_like(weights)
-    groups = TILES // GROUP
-    for n in range(groups):
-        for c in range(2 * GROUP):
-            q = rounded[layers[n * GROUP + c // 2]]
-            h = c % 2
-            weights[n, c * 8 : c * 8 + 8, h * LANES : (h + 1) * LANES] = jnp.concatenate([q, q], 0)
-    lane = lax.broadcasted_iota(jnp.int32, (LANES, LANES), 1)
+    zero = jnp.zeros((4, LANES), F32)
+    for layer in range(len(SIZES)):
+        q = rounded[layer]
+        rows = (jnp.concatenate([q, zero], 1), jnp.concatenate([zero, q], 1))
+        none = jnp.zeros((4, 2 * LANES), F32)
+        weights[layer, 0] = jnp.concatenate([rows[0], none, rows[1], none], 0)
+        weights[layer, 1] = jnp.concatenate([none, rows[0], none, rows[1]], 0)
 
     def copy(n):
-        rows = pl.ds(n * GROUP * TILE, GROUP * TILE)
+        rows = pl.ds(n * PIECE * TILE, PIECE * TILE)
         return pltpu.make_async_copy(obuf.at[rows], out_hbm.at[0, rows], sems.at[n])
 
-    def group(n, _):
-        w = weights[n].astype(BF16)
+    for n in range(TILES // GROUP):
         left = turned[n]
         for k in range(GROUP):
+            t = n * GROUP + k
             for other in range(2):
-                chosen = (lane // 16 == k) & ((lane // 4) % 2 == other)
-                update = jnp.dot(
-                    jnp.where(chosen, left, jnp.zeros_like(left)), w, preferred_element_type=F32
-                )
+                w = weights[layers[t], other].astype(BF16)
+                parts = [w]
+                if k:
+                    parts.insert(0, jnp.zeros((16 * k, 2 * LANES), BF16))
+                if k < GROUP - 1:
+                    parts.append(jnp.zeros((LANES - 16 * (k + 1), 2 * LANES), BF16))
+                update = jnp.dot(left, jnp.concatenate(parts, 0), preferred_element_type=F32)
                 which = own if other == 0 else 1 - own
-                at = pl.multiple_of((n * GROUP + k) * TILE + which * HALF, HALF)
+                at = pl.multiple_of(t * TILE + which * HALF, HALF)
                 for h in range(2):
                     rows = pl.ds(pl.multiple_of(at + h * LANES, LANES), LANES)
                     obuf[rows] = (
                         comp[rows].astype(F32) - update[:, h * LANES : (h + 1) * LANES]
                     ).astype(BF16)
-        copy(n).start()
-
-    lax.fori_loop(0, groups, group, None)
-    for n in range(groups):
+            if t % PIECE == PIECE - 1:
+                copy(t // PIECE).start()
+    for n in range(PIECES):
         copy(n).wait()
 
 
-def new_residual(scalars, q_mine, q_other, turned, comp):
+def new_residual(q_mine, q_other, turned, comp):
     return pl.pallas_call(
         residual_kernel,
         out_shape=(
             jax.ShapeDtypeStruct((1, ROWS, LANES), BF16),
             jax.ShapeDtypeStruct((len(SIZES), 4, LANES), F32),
         ),
-        in_specs=[SM, VM, VM, VM, VM],
+        in_specs=[VM, VM, VM, VM],
         out_specs=(HB, VM),
         scratch_shapes=[
-            pltpu.VMEM((TILES // GROUP, LANES, 2 * LANES), F32),
+            pltpu.VMEM((len(SIZES), 2, 16, 2 * LANES), F32),
             pltpu.VMEM((ROWS, LANES), BF16),
-            pltpu.SemaphoreType.DMA((TILES // GROUP,)),
+            pltpu.SemaphoreType.DMA((PIECES,)),
         ],
         compiler_params=pltpu.CompilerParams(vmem_limit_bytes=24 * MIB),
         name="new_residual",
-    )(scalars, q_mine, q_other, turned, comp)
+    )(q_mine, q_other, turned, comp)
 
 
 def body(grad, residual, q_prev, owner_table):
-    own = lax.axis_index("grp").astype(jnp.int32)
-    place = lax.axis_index("dp").astype(jnp.int32)
-    scalars = jnp.concatenate([jnp.stack([own, place]), owner_table])
-    comp, keep, send = project(scalars, grad, residual, q_prev)
+    comp, keep, send = project(grad, residual, q_prev)
     both = keep + lax.ppermute(send, "grp", SWAP)
     arrived = lax.all_to_all(both, "dp", 0, 0, tiled=True)
     mine = lax.all_to_all(spread(arrived), "dp", 0, 0, tiled=True)
     other = lax.ppermute(mine, "grp", SWAP)
-    owned, q_part, turned = orthonormal_bases(scalars, mine, other, comp)
+    owned, q_part, turned = orthonormal_bases(owner_table, mine, other, comp)
     q_there = lax.ppermute(q_part, "grp", SWAP)
-    out, q_new = new_residual(scalars, q_part, q_there, turned, comp)
+    out, q_new = new_residual(q_part, q_there, turned, comp)
     return out, q_new, owned
 
 

time: 64.1 us -> 61.5 us (0.959)
  local copies, waits for them, and re-layouts: 4.08 us -> 0.01 us
  Pallas kernels: 15.3 us -> 17.7 us
  other arithmetic: 0.8 us -> 0.07 us
    unnamed x4 -> x2, local copies, waits for them, and re-layouts: 4.08 us -> 0.01 us
    pallas_call x1, Pallas kernels: 6.71 us -> 10.5 us  [project(): pl.pallas_call(project_kernel, out_shape=(pltpu.VMEM((ROWS, LANES), BF16)...]
    pallas_call x1, Pallas kernels: 5.82 us -> 4.28 us  [new_residual(): pl.pallas_call(residual_kernel, out_shape=(jax.ShapeDtypeStruct((1, ROWS,...]
    concatenate x1 -> x0, other arithmetic: 0.73 us -> none  [body(): scalars = jnp.concatenate([jnp.stack([own, place]), owner_table])]
where the time goes in v2:
time: 61.5 us; the launch traced here: 61.4 us
  blocking collectives  34.8 us (57%)
  Pallas kernels  17.7 us (29%)
  starting transfers between devices  4.97 us (8%)
  waiting for transfers between devices  3.16 us (5%)
  between operations  0.67 us (1%)
    all_to_all x1, blocking collectives, body(): arrived = lax.all_to_all(both, 'dp', 0, 0, tiled=True)  21 us
    all_to_all x1, blocking collectives, body(): mine = lax.all_to_all(spread(arrived), 'dp', 0, 0, tiled=True)  13.8 us
    pallas_call x1, Pallas kernels, project(): pl.pallas_call(project_kernel, out_shape=(pltpu.VMEM((ROWS, LANES), BF16)...  10.5 us
    pallas_call x1, Pallas kernels, new_residual(): pl.pallas_call(residual_kernel, out_shape=(jax.ShapeDtypeStruct((1, ROWS,...  4.28 us
    ppermute x1, starting transfers between devices, body(): other = lax.ppermute(mine, 'grp', SWAP)  3.06 us
    pallas_call x1, Pallas kernels, orthonormal_bases(): pl.pallas_call(basis_kernel, out_shape=(jax.ShapeDtypeStruct((1, 4, max(S...  2.84 us
    ppermute x1, starting transfers between devices, body(): both = keep + lax.ppermute(send, 'grp', SWAP)  1.46 us
  transfers between devices with their start and end apart: 3, of which 3 were waited for; matrix products, arithmetic and copies ran while one was open for 0% of the time, Pallas kernels for 0%

profile of v2, /device:TPU:1, one launch (start us, length us, event | category | flops | bytes accessed | tf_op | source)
XLA Modules:
  0.0 61.4 jit_solution(2149653270149807304)
XLA Ops:
  0.6 0.0 copy-start
  0.6 10.5 %project.1 = (bf16[32768,128]{1,0:T(8,128)(2,1)S(1)}, f32[64,4,256]{2,1,0:T(4,128)S(1)}, f32[64,4,256]{2,1,0:T(4,128)S(1)}) custom-call(bf16[1,32768,128]{2,1,0:T(8,128)(2,1)} %grad.1, bf16[1,32768,128]{2,1,0:T(8,128)(2,1)} %residual.1, f32[5,4,128]{2,1,0:T(4,128)} %q_hbm.1), custom_call_target="tpu_custom_call" | custom-call | tf_op jit(solution)/shard_map/project/pallas_call | solution.py:110
  11.2 1.5 %collective-permute-start = (f32[64,4,256]{2,1,0:T(4,128)S(1)}, f32[64,4,256]{2,1,0:T(4,128)S(1)}, u32[]{:S(2)}, u32[]{:S(2)}) collective-permute-start(f32[64,4,256]{2,1,0:T(4,128)S(1)} %get-tuple-element.12), channel_id=1, source_target_pairs={{0,64},{64,0},{1,65},{65,1},{2,66},{66,2},{3,67},{67,3},{4,68},{68... | collective-permute-start | bytes 786440 | tf_op jit(solution)/shard_map/ppermute | solution.py:341
  12.6 1.2 %collective-permute-done = f32[64,4,256]{2,1,0:T(4,128)S(1)} collective-permute-done((f32[64,4,256]{2,1,0:T(4,128)S(1)}, f32[64,4,256]{2,1,0:T(4,128)S(1)}, u32[]{:S(2)}, u32[]{:S(2)}) %collective-permute-start) | collective-permute-done | bytes 262176 | tf_op jit(solution)/shard_map/ppermute | solution.py:341
  13.8 0.1 add.3
  13.9 21.0 %all_to_all.10.x_ref = f32[64,4,256]{2,1,0:T(4,128)S(1)} all-to-all(f32[64,4,256]{2,1,0:T(4,128)S(1)} %add.3), channel_id=1, replica_groups=mesh['grp'=2,'dp'=64] {'dp'}, dimensions={0} | all-to-all | bytes 524288 | tf_op jit(solution)/shard_map/all_to_all | solution.py:342
  34.8 0.1 spread.1
  34.9 13.8 %all_to_all.11.mine = f32[64,4,256]{2,1,0:T(4,128)S(1)} all-to-all(f32[64,4,256]{2,1,0:T(4,128)S(1)} %spread.1), channel_id=1, replica_groups=mesh['grp'=2,'dp'=64] {'dp'}, dimensions={0} | all-to-all | bytes 524288 | tf_op jit(solution)/shard_map/all_to_all | solution.py:343
  48.7 3.1 %collective-permute-start.1 = (f32[64,4,256]{2,1,0:T(4,128)S(1)}, f32[64,4,256]{2,1,0:T(4,128)S(1)}, u32[]{:S(2)}, u32[]{:S(2)}) collective-permute-start(f32[64,4,256]{2,1,0:T(4,128)S(1)} %all_to_all.11.mine), channel_id=1, source_target_pairs={{0,64},{64,0},{1,65},{65,1},{2,66},{66,2},{3,67},{67,3},{4,68},{68... | collective-permute-start | bytes 786440 | tf_op jit(solution)/shard_map/ppermute | solution.py:344
  51.8 1.2 %collective-permute-done.1.other = f32[64,4,256]{2,1,0:T(4,128)S(1)} collective-permute-done((f32[64,4,256]{2,1,0:T(4,128)S(1)}, f32[64,4,256]{2,1,0:T(4,128)S(1)}, u32[]{:S(2)}, u32[]{:S(2)}) %collective-permute-start.1) | collective-permute-done | bytes 262176 | tf_op jit(solution)/shard_map/ppermute | solution.py:344
  53.0 0.0 copy-done
  53.0 2.8 %bases.1 = (f32[1,4,14336]{2,1,0:T(4,128)}, f32[5,4,128]{2,1,0:T(4,128)S(1)}, bf16[8,128,128]{2,1,0:T(8,128)(2,1)S(1)}) custom-call(s32[5]{0:T(128)S(1)} %copy-done, f32[64,4,256]{2,1,0:T(4,128)S(1)} %all_to_all.11.mine, f32[64,4,256]{2,1,0:T(4,128)S(1)} %collective-permute-done.1.other, bf16[32768,128]{1,0:T(8,128)(2,1)S(1)} %get-tuple-element.13.comp), custom_call_target="tpu_custom_call" | custom-call | tf_op jit(solution)/shard_map/bases/pallas_call | solution.py:253
  55.8 0.5 collective-permute-start.2
  56.3 0.8 %collective-permute-done.2.q_other = f32[5,4,128]{2,1,0:T(4,128)S(1)} collective-permute-done((f32[5,4,128]{2,1,0:T(4,128)S(1)}, f32[5,4,128]{2,1,0:T(4,128)S(1)}, u32[]{:S(2)}, u32[]{:S(2)}) %collective-permute-start.2) | collective-permute-done | bytes 10272 | tf_op jit(solution)/shard_map/ppermute | solution.py:346
  57.1 4.3 %new_residual.1 = (bf16[1,32768,128]{2,1,0:T(8,128)(2,1)}, f32[5,4,128]{2,1,0:T(4,128)}) custom-call(f32[5,4,128]{2,1,0:T(4,128)S(1)} %get-tuple-element.14.q_mine, f32[5,4,128]{2,1,0:T(4,128)S(1)} %collective-permute-done.2.q_other, bf16[8,128,128]{2,1,0:T(8,128)(2,1)S(1)} %get-tuple-element.15.turned, bf16[32768,128]{1,0:T(8,128)(2,1)S(1)} %get-tuple-element.13.comp), custom_call_target="tpu_custom_call" | custom-call | tf_op jit(solution)/shard_map/new_residual/pallas_call | solution.py:321
Async XLA Ops:
  0.6 52.3 %copy-start = (s32[5]{0:T(128)S(1)}, s32[5]{0:T(128)}, u32[]{:S(2)}) copy-start(s32[5]{0:T(128)} %owner.1) | copy-start | bytes 64
  11.2 2.6 %collective-permute-start = (f32[64,4,256]{2,1,0:T(4,128)S(1)}, f32[64,4,256]{2,1,0:T(4,128)S(1)}, u32[]{:S(2)}, u32[]{:S(2)}) collective-permute-start(f32[64,4,256]{2,1,0:T(4,128)S(1)} %get-tuple-element.12), channel_id=1, source_target_pairs={{0,64},{64,0},{1,65},{65,1},{2,66},{66,2},{3,67},{67,3},{4,68},{68... | collective-permute-start | bytes 786440 | tf_op jit(solution)/shard_map/ppermute | solution.py:341
  48.7 4.2 %collective-permute-start.1 = (f32[64,4,256]{2,1,0:T(4,128)S(1)}, f32[64,4,256]{2,1,0:T(4,128)S(1)}, u32[]{:S(2)}, u32[]{:S(2)}) collective-permute-start(f32[64,4,256]{2,1,0:T(4,128)S(1)} %all_to_all.11.mine), channel_id=1, source_target_pairs={{0,64},{64,0},{1,65},{65,1},{2,66},{66,2},{3,67},{67,3},{4,68},{68... | collective-permute-start | bytes 786440 | tf_op jit(solution)/shard_map/ppermute | solution.py:344
  55.8 1.3 %collective-permute-start.2 = (f32[5,4,128]{2,1,0:T(4,128)S(1)}, f32[5,4,128]{2,1,0:T(4,128)S(1)}, u32[]{:S(2)}, u32[]{:S(2)}) collective-permute-start(f32[5,4,128]{2,1,0:T(4,128)S(1)} %get-tuple-element.14.q_mine), channel_id=1, source_target_pairs={{0,64},{64,0},{1,65},{65,1},{2,66},{66,2},{3,67},{67,3},{4,68},{68... | collective-permute-start | bytes 30728 | tf_op jit(solution)/shard_map/ppermute | solution.py:346

commit v3 on v2

--- a/solution.py
+++ b/solution.py
@@ -40,14 +40,15 @@
 HB = pl.BlockSpec(memory_space=pltpu.HBM)
 
 
-CHUNK_TILES = 4
-CHUNK = CHUNK_TILES * TILE
-CHUNKS = ROWS // CHUNK
+CHUNKS = (16, 16, 16, 8, 4, 4)
+DEPTH = 3
 
 
 def project_kernel(grad, residual, q_hbm, comp_ref, keep_ref, send_ref, gbuf, rbuf, q_ref, lhs, sems, q_sem):
+    firsts = [sum(CHUNKS[:c]) for c in range(len(CHUNKS))]
+
     def copies(c):
-        rows = pl.ds(c * CHUNK, CHUNK)
+        rows = pl.ds(firsts[c] * TILE, CHUNKS[c] * TILE)
         return (
             pltpu.make_async_copy(grad.at[0, rows], gbuf.at[rows], sems.at[0, c]),
             pltpu.make_async_copy(residual.at[0, rows], rbuf.at[rows], sems.at[1, c]),
@@ -55,7 +56,7 @@
 
     q_copy = pltpu.make_async_copy(q_hbm, q_ref, q_sem)
     q_copy.start()
-    for c in range(CHUNKS):
+    for c in range(DEPTH):
         for copy in copies(c):
             copy.start()
     own = lax.axis_index("grp")
@@ -71,38 +72,28 @@
         )
         lhs[layer] = jnp.where(own == 0, straight, crossed)
 
-    def chunk(c, layers):
+    layers = tile_layers()
+    for c, count in enumerate(CHUNKS):
         for copy in copies(c):
             copy.wait()
-        for k in range(CHUNK_TILES):
-            t = c * CHUNK_TILES + k
+        if c + DEPTH < len(CHUNKS):
+            for copy in copies(c + DEPTH):
+                copy.start()
+        for t in range(firsts[c], firsts[c] + count):
             halves = []
             for h in range(2):
-                rows = pl.ds(pl.multiple_of(t * TILE + h * HALF, HALF), HALF)
+                rows = slice(t * TILE + h * HALF, t * TILE + (h + 1) * HALF)
                 value = (gbuf[rows].astype(F32) + rbuf[rows].astype(F32)).astype(BF16)
                 comp_ref[rows] = value
                 halves.append(value)
             out = lax.dot_general(
-                lhs[layers[k]].astype(BF16),
+                lhs[layers[t]].astype(BF16),
                 jnp.concatenate(halves, 1),
                 (((1,), (1,)), ((), ())),
                 preferred_element_type=F32,
             )
             keep_ref[t] = out[:4]
             send_ref[t] = out[4:]
-
-    layers = tile_layers()
-    groups = [tuple(layers[c * CHUNK_TILES : (c + 1) * CHUNK_TILES]) for c in range(CHUNKS)]
-    c = 0
-    while c < CHUNKS:
-        end = c
-        while end < CHUNKS and groups[end] == groups[c]:
-            end += 1
-        if end - c == 1:
-            chunk(c, groups[c])
-        else:
-            lax.fori_loop(c, end, lambda i, _, now=groups[c]: chunk(i, now), None)
-        c = end
 
 
 def project(grad, residual, q_prev):
@@ -117,7 +108,7 @@
             pltpu.VMEM((ROWS, LANES), BF16),
             pltpu.VMEM((len(SIZES), 4, LANES), F32),
             pltpu.VMEM((len(SIZES), 8, 2 * LANES), F32),
-            pltpu.SemaphoreType.DMA((2, CHUNKS)),
+            pltpu.SemaphoreType.DMA((2, len(CHUNKS))),
             pltpu.SemaphoreType.DMA,
         ],
         compiler_params=pltpu.CompilerParams(vmem_limit_bytes=30 * MIB),
@@ -192,26 +183,10 @@
     return columns
 
 
-def basis_kernel(owner, mine, other, comp, owned_hbm, q_ref, turned_ref, joined, stacked, owned, sem):
-    own, place = lax.axis_index("grp"), lax.axis_index("dp")
+def basis_kernel(mine, other, comp, q_ref, turned_ref, joined, stacked):
+    own = lax.axis_index("grp")
     counts = [rows // TILE for rows in SIZES]
     starts = layer_starts()
-
-    owned[...] = jnp.zeros_like(owned)
-    for layer, count in enumerate(counts):
-
-        @pl.when(owner[layer] == place)
-        def _():
-            def step(k, _):
-                at = pl.multiple_of(k * TILE + own * HALF, HALF)
-                owned[0, :, pl.ds(at, HALF)] = mine[starts[layer] + k]
-                at = pl.multiple_of(k * TILE + (1 - own) * HALF, HALF)
-                owned[0, :, pl.ds(at, HALF)] = other[starts[layer] + k]
-
-            lax.fori_loop(0, count, step, None)
-
-    copy = pltpu.make_async_copy(owned, owned_hbm, sem)
-    copy.start()
 
     grams = []
     for layer, count in enumerate(counts):
@@ -246,36 +221,52 @@
         q_ref[layer] = total[:4, :LANES] + total[4:, LANES:]
     for n in range(TILES // GROUP):
         turned_ref[n] = stacked[n].T.astype(BF16)
-    copy.wait()
-
-
-def orthonormal_bases(owner_table, mine, other, comp):
+
+
+def orthonormal_bases(mine, other, comp):
     return pl.pallas_call(
         basis_kernel,
         out_shape=(
-            jax.ShapeDtypeStruct((1, 4, max(SIZES)), F32),
             jax.ShapeDtypeStruct((len(SIZES), 4, LANES), F32),
             pltpu.VMEM((TILES // GROUP, LANES, LANES), BF16),
         ),
-        in_specs=[SM, VM, VM, VM],
-        out_specs=(HB, VM, VM),
+        in_specs=[VM, VM, VM],
+        out_specs=(VM, VM),
         scratch_shapes=[
             pltpu.VMEM((TILES, 8, HALF), F32),
             pltpu.VMEM((TILES // GROUP, LANES, LANES), F32),
-            pltpu.VMEM((1, 4, max(SIZES)), F32),
-            pltpu.SemaphoreType.DMA,
         ],
         compiler_params=pltpu.CompilerParams(vmem_limit_bytes=16 * MIB),
         name="bases",
-    )(owner_table, mine, other, comp)
+    )(mine, other, comp)
 
 
 PIECE = 4
 PIECES = TILES // PIECE
 
 
-def residual_kernel(q_mine, q_other, turned, comp, out_hbm, q_ref, weights, obuf, sems):
-    own = lax.axis_index("grp")
+def residual_kernel(
+    owner, q_mine, q_other, turned, comp, mine, other_half, out_hbm, q_ref, owned_hbm, weights, obuf, owned, sems
+):
+    own, place = lax.axis_index("grp"), lax.axis_index("dp")
+    owned_copy = pltpu.make_async_copy(owned, owned_hbm, sems.at[PIECES])
+
+    def write_owned():
+        owned[...] = jnp.zeros_like(owned)
+        for layer, first in enumerate(layer_starts()):
+
+            @pl.when(owner[layer] == place)
+            def _():
+                def step(k, _):
+                    at = pl.multiple_of(k * TILE + own * HALF, HALF)
+                    owned[0, :, pl.ds(at, HALF)] = mine[first + k]
+                    at = pl.multiple_of(k * TILE + (1 - own) * HALF, HALF)
+                    owned[0, :, pl.ds(at, HALF)] = other_half[first + k]
+
+                lax.fori_loop(0, SIZES[layer] // TILE, step, None)
+
+        owned_copy.start()
+
     layers = tile_layers()
     q_new = (q_mine[...] + q_other[...]) * 0.5
     q_ref[...] = q_new
@@ -313,27 +304,32 @@
                     ).astype(BF16)
             if t % PIECE == PIECE - 1:
                 copy(t // PIECE).start()
+        if n == 1:
+            write_owned()
+    owned_copy.wait()
     for n in range(PIECES):
         copy(n).wait()
 
 
-def new_residual(q_mine, q_other, turned, comp):
+def new_residual(owner_table, q_mine, q_other, turned, comp, mine, other):
     return pl.pallas_call(
         residual_kernel,
         out_shape=(
             jax.ShapeDtypeStruct((1, ROWS, LANES), BF16),
             jax.ShapeDtypeStruct((len(SIZES), 4, LANES), F32),
+            jax.ShapeDtypeStruct((1, 4, max(SIZES)), F32),
         ),
-        in_specs=[VM, VM, VM, VM],
-        out_specs=(HB, VM),
+        in_specs=[SM, VM, VM, VM, VM, VM, VM],
+        out_specs=(HB, VM, HB),
         scratch_shapes=[
             pltpu.VMEM((len(SIZES), 2, 16, 2 * LANES), F32),
             pltpu.VMEM((ROWS, LANES), BF16),
-            pltpu.SemaphoreType.DMA((PIECES,)),
+            pltpu.VMEM((1, 4, max(SIZES)), F32),
+            pltpu.SemaphoreType.DMA((PIECES + 1,)),
         ],
         compiler_params=pltpu.CompilerParams(vmem_limit_bytes=24 * MIB),
         name="new_residual",
-    )(q_mine, q_other, turned, comp)
+    )(owner_table, q_mine, q_other, turned, comp, mine, other)
 
 
 def body(grad, residual, q_prev, owner_table):
@@ -342,10 +338,9 @@
     arrived = lax.all_to_all(both, "dp", 0, 0, tiled=True)
     mine = lax.all_to_all(spread(arrived), "dp", 0, 0, tiled=True)
     other = lax.ppermute(mine, "grp", SWAP)
-    owned, q_part, turned = orthonormal_bases(owner_table, mine, other, comp)
+    q_part, turned = orthonormal_bases(mine, other, comp)
     q_there = lax.ppermute(q_part, "grp", SWAP)
-    out, q_new = new_residual(q_part, q_there, turned, comp)
-    return out, q_new, owned
+    return new_residual(owner_table, q_part, q_there, turned, comp, mine, other)
 
 
 def solution(mesh):

time: 61.5 us -> 57.3 us (0.932)
  Pallas kernels: 17.7 us -> 13.6 us
    pallas_call x1, Pallas kernels: 10.5 us -> 6.86 us  [project(): pl.pallas_call(project_kernel, out_shape=(pltpu.VMEM((ROWS, LANES), BF16)...]
    pallas_call x1, Pallas kernels: 2.84 us -> 1.64 us  [orthonormal_bases(): pl.pallas_call(basis_kernel, out_shape=(jax.ShapeDtypeStruct((len(SIZES),...]
    pallas_call x1, Pallas kernels: 4.28 us -> 5.01 us  [new_residual(): pl.pallas_call(residual_kernel, out_shape=(jax.ShapeDtypeStruct((1, ROWS,...]
where the time goes in v3:
time: 57.3 us; the launch traced here: 57.2 us
  blocking collectives  34.8 us (61%)
  Pallas kernels  13.6 us (24%)
  starting transfers between devices  4.92 us (9%)
  waiting for transfers between devices  3.16 us (6%)
  between operations  0.66 us (1%)
    all_to_all x1, blocking collectives, body(): arrived = lax.all_to_all(both, 'dp', 0, 0, tiled=True)  21 us
    all_to_all x1, blocking collectives, body(): mine = lax.all_to_all(spread(arrived), 'dp', 0, 0, tiled=True)  13.8 us
    pallas_call x1, Pallas kernels, project(): pl.pallas_call(project_kernel, out_shape=(pltpu.VMEM((ROWS, LANES), BF16)...  6.86 us
    pallas_call x1, Pallas kernels, new_residual(): pl.pallas_call(residual_kernel, out_shape=(jax.ShapeDtypeStruct((1, ROWS,...  5.01 us
    ppermute x1, starting transfers between devices, body(): other = lax.ppermute(mine, 'grp', SWAP)  3.06 us
    pallas_call x1, Pallas kernels, orthonormal_bases(): pl.pallas_call(basis_kernel, out_shape=(jax.ShapeDtypeStruct((len(SIZES),...  1.64 us
    ppermute x1, starting transfers between devices, body(): both = keep + lax.ppermute(send, 'grp', SWAP)  1.46 us
    ppermute x1, waiting for transfers between devices, body(): both = keep + lax.ppermute(send, 'grp', SWAP)  1.16 us
  transfers between devices with their start and end apart: 3, of which 3 were waited for; matrix products, arithmetic and copies ran while one was open for 0% of the time, Pallas kernels for 0%

profile of v3, /device:TPU:1, one launch (start us, length us, event | category | flops | bytes accessed | tf_op | source)
XLA Modules:
  0.0 57.2 jit_solution(9319169067751524039)
XLA Ops:
  0.6 6.9 %project.1 = (bf16[32768,128]{1,0:T(8,128)(2,1)S(1)}, f32[64,4,256]{2,1,0:T(4,128)S(1)}, f32[64,4,256]{2,1,0:T(4,128)S(1)}) custom-call(bf16[1,32768,128]{2,1,0:T(8,128)(2,1)} %grad.1, bf16[1,32768,128]{2,1,0:T(8,128)(2,1)} %residual.1, f32[5,4,128]{2,1,0:T(4,128)} %q_hbm.1), custom_call_target="tpu_custom_call" | custom-call | tf_op jit(solution)/shard_map/project/pallas_call | solution.py:101
  7.5 0.0 copy-start
  7.5 1.5 %collective-permute-start = (f32[64,4,256]{2,1,0:T(4,128)S(1)}, f32[64,4,256]{2,1,0:T(4,128)S(1)}, u32[]{:S(2)}, u32[]{:S(2)}) collective-permute-start(f32[64,4,256]{2,1,0:T(4,128)S(1)} %get-tuple-element.9), channel_id=1, source_target_pairs={{0,64},{64,0},{1,65},{65,1},{2,66},{66,2},{3,67},{67,3},{4,68},{68... | collective-permute-start | bytes 786440 | tf_op jit(solution)/shard_map/ppermute | solution.py:337
  9.0 1.2 %collective-permute-done = f32[64,4,256]{2,1,0:T(4,128)S(1)} collective-permute-done((f32[64,4,256]{2,1,0:T(4,128)S(1)}, f32[64,4,256]{2,1,0:T(4,128)S(1)}, u32[]{:S(2)}, u32[]{:S(2)}) %collective-permute-start) | collective-permute-done | bytes 262176 | tf_op jit(solution)/shard_map/ppermute | solution.py:337
  10.1 0.1 add.3
  10.2 21.0 %all_to_all.10.x_ref = f32[64,4,256]{2,1,0:T(4,128)S(1)} all-to-all(f32[64,4,256]{2,1,0:T(4,128)S(1)} %add.3), channel_id=1, replica_groups=mesh['grp'=2,'dp'=64] {'dp'}, dimensions={0} | all-to-all | bytes 524288 | tf_op jit(solution)/shard_map/all_to_all | solution.py:338
  31.2 0.1 spread.1
  31.2 13.8 %all_to_all.11.mine = f32[64,4,256]{2,1,0:T(4,128)S(1)} all-to-all(f32[64,4,256]{2,1,0:T(4,128)S(1)} %spread.1), channel_id=1, replica_groups=mesh['grp'=2,'dp'=64] {'dp'}, dimensions={0} | all-to-all | bytes 524288 | tf_op jit(solution)/shard_map/all_to_all | solution.py:339
  45.1 3.1 %collective-permute-start.1 = (f32[64,4,256]{2,1,0:T(4,128)S(1)}, f32[64,4,256]{2,1,0:T(4,128)S(1)}, u32[]{:S(2)}, u32[]{:S(2)}) collective-permute-start(f32[64,4,256]{2,1,0:T(4,128)S(1)} %all_to_all.11.mine), channel_id=1, source_target_pairs={{0,64},{64,0},{1,65},{65,1},{2,66},{66,2},{3,67},{67,3},{4,68},{68... | collective-permute-start | bytes 786440 | tf_op jit(solution)/shard_map/ppermute | solution.py:340
  48.1 1.2 %collective-permute-done.1.other.other_half = f32[64,4,256]{2,1,0:T(4,128)S(1)} collective-permute-done((f32[64,4,256]{2,1,0:T(4,128)S(1)}, f32[64,4,256]{2,1,0:T(4,128)S(1)}, u32[]{:S(2)}, u32[]{:S(2)}) %collective-permute-start.1) | collective-permute-done | bytes 262176 | tf_op jit(solution)/shard_map/ppermute | solution.py:340
  49.3 1.6 %bases.1 = (f32[5,4,128]{2,1,0:T(4,128)S(1)}, bf16[8,128,128]{2,1,0:T(8,128)(2,1)S(1)}) custom-call(f32[64,4,256]{2,1,0:T(4,128)S(1)} %all_to_all.11.mine, f32[64,4,256]{2,1,0:T(4,128)S(1)} %collective-permute-done.1.other.other_half, bf16[32768,128]{1,0:T(8,128)(2,1)S(1)} %get-tuple-element.10.comp), custom_call_target="tpu_custom_call" | custom-call | tf_op jit(solution)/shard_map/bases/pallas_call | solution.py:227
  50.9 0.4 collective-permute-start.2
  51.3 0.8 %collective-permute-done.2.q_other = f32[5,4,128]{2,1,0:T(4,128)S(1)} collective-permute-done((f32[5,4,128]{2,1,0:T(4,128)S(1)}, f32[5,4,128]{2,1,0:T(4,128)S(1)}, u32[]{:S(2)}, u32[]{:S(2)}) %collective-permute-start.2) | collective-permute-done | bytes 10272 | tf_op jit(solution)/shard_map/ppermute | solution.py:342
  52.2 0.0 copy-done
  52.2 5.0 %new_residual.1 = (bf16[1,32768,128]{2,1,0:T(8,128)(2,1)}, f32[5,4,128]{2,1,0:T(4,128)}, f32[1,4,14336]{2,1,0:T(4,128)}) custom-call(s32[5]{0:T(128)S(1)} %copy-done, f32[5,4,128]{2,1,0:T(4,128)S(1)} %get-tuple-element.11.q_mine, f32[5,4,128]{2,1,0:T(4,128)S(1)} %collective-permute-done.2.q_other, bf16[8,128,128]{2,1,0:T(8,128)(2,1)S(1)} %get-tuple-element.12.turned, ...), custom_call_target="tpu_custom_call" | custom-call | tf_op jit(solution)/shard_map/new_residual/pallas_call | solution.py:315
Async XLA Ops:
  7.5 44.7 %copy-start = (s32[5]{0:T(128)S(1)}, s32[5]{0:T(128)}, u32[]{:S(2)}) copy-start(s32[5]{0:T(128)} %owner.1) | copy-start | bytes 64
  7.5 2.6 %collective-permute-start = (f32[64,4,256]{2,1,0:T(4,128)S(1)}, f32[64,4,256]{2,1,0:T(4,128)S(1)}, u32[]{:S(2)}, u32[]{:S(2)}) collective-permute-start(f32[64,4,256]{2,1,0:T(4,128)S(1)} %get-tuple-element.9), channel_id=1, source_target_pairs={{0,64},{64,0},{1,65},{65,1},{2,66},{66,2},{3,67},{67,3},{4,68},{68... | collective-permute-start | bytes 786440 | tf_op jit(solution)/shard_map/ppermute | solution.py:337
  45.1 4.2 %collective-permute-start.1 = (f32[64,4,256]{2,1,0:T(4,128)S(1)}, f32[64,4,256]{2,1,0:T(4,128)S(1)}, u32[]{:S(2)}, u32[]{:S(2)}) collective-permute-start(f32[64,4,256]{2,1,0:T(4,128)S(1)} %all_to_all.11.mine), channel_id=1, source_target_pairs={{0,64},{64,0},{1,65},{65,1},{2,66},{66,2},{3,67},{67,3},{4,68},{68... | collective-permute-start | bytes 786440 | tf_op jit(solution)/shard_map/ppermute | solution.py:340
  50.9 1.2 %collective-permute-start.2 = (f32[5,4,128]{2,1,0:T(4,128)S(1)}, f32[5,4,128]{2,1,0:T(4,128)S(1)}, u32[]{:S(2)}, u32[]{:S(2)}) collective-permute-start(f32[5,4,128]{2,1,0:T(4,128)S(1)} %get-tuple-element.11.q_mine), channel_id=1, source_target_pairs={{0,64},{64,0},{1,65},{65,1},{2,66},{66,2},{3,67},{67,3},{4,68},{68... | collective-permute-start | bytes 30728 | tf_op jit(solution)/shard_map/ppermute | solution.py:342

commit v4 on v3

--- a/solution.py
+++ b/solution.py
@@ -36,11 +36,10 @@
 
 
 VM = pl.BlockSpec(memory_space=pltpu.VMEM)
-SM = pl.BlockSpec(memory_space=pltpu.SMEM)
 HB = pl.BlockSpec(memory_space=pltpu.HBM)
 
 
-CHUNKS = (16, 16, 16, 8, 4, 4)
+CHUNKS = (8, 16, 24, 8, 4, 4)
 DEPTH = 3
 
 
@@ -246,12 +245,18 @@
 
 
 def residual_kernel(
-    owner, q_mine, q_other, turned, comp, mine, other_half, out_hbm, q_ref, owned_hbm, weights, obuf, owned, sems
+    owner_hbm, q_mine, q_other, turned, comp, mine, other_half,
+    out_hbm, q_hbm, owned_hbm,
+    weights, obuf, owned, q_ref, owner, sems,
 ):
     own, place = lax.axis_index("grp"), lax.axis_index("dp")
     owned_copy = pltpu.make_async_copy(owned, owned_hbm, sems.at[PIECES])
+    q_copy = pltpu.make_async_copy(q_ref, q_hbm, sems.at[PIECES + 1])
+    owner_copy = pltpu.make_async_copy(owner_hbm, owner, sems.at[PIECES + 2])
+    owner_copy.start()
 
     def write_owned():
+        owner_copy.wait()
         owned[...] = jnp.zeros_like(owned)
         for layer, first in enumerate(layer_starts()):
 
@@ -270,6 +275,7 @@
     layers = tile_layers()
     q_new = (q_mine[...] + q_other[...]) * 0.5
     q_ref[...] = q_new
+    q_copy.start()
     rounded = q_new.astype(BF16).astype(F32)
     zero = jnp.zeros((4, LANES), F32)
     for layer in range(len(SIZES)):
@@ -304,9 +310,10 @@
                     ).astype(BF16)
             if t % PIECE == PIECE - 1:
                 copy(t // PIECE).start()
-        if n == 1:
+        if n == TILES // GROUP - 1:
             write_owned()
     owned_copy.wait()
+    q_copy.wait()
     for n in range(PIECES):
         copy(n).wait()
 
@@ -319,17 +326,22 @@
             jax.ShapeDtypeStruct((len(SIZES), 4, LANES), F32),
             jax.ShapeDtypeStruct((1, 4, max(SIZES)), F32),
         ),
-        in_specs=[SM, VM, VM, VM, VM, VM, VM],
-        out_specs=(HB, VM, HB),
+        in_specs=[HB, VM, VM, VM, VM, VM, VM],
+        out_specs=(HB, HB, HB),
         scratch_shapes=[
             pltpu.VMEM((len(SIZES), 2, 16, 2 * LANES), F32),
             pltpu.VMEM((ROWS, LANES), BF16),
             pltpu.VMEM((1, 4, max(SIZES)), F32),
-            pltpu.SemaphoreType.DMA((PIECES + 1,)),
+            pltpu.VMEM((len(SIZES), 4, LANES), F32),
+            pltpu.SMEM((len(SIZES),), jnp.int32),
+            pltpu.SemaphoreType.DMA((PIECES + 3,)),
         ],
         compiler_params=pltpu.CompilerParams(vmem_limit_bytes=24 * MIB),
         name="new_residual",
-    )(owner_table, q_mine, q_other, turned, comp, mine, other)
+    )(
+        pltpu.with_memory_space_constraint(owner_table, pltpu.HBM),
+        q_mine, q_other, turned, comp, mine, other,
+    )
 
 
 def body(grad, residual, q_prev, owner_table):

time: 57.3 us -> 55.9 us (0.976)
  Pallas kernels: 13.6 us -> 12.2 us
    pallas_call x1, Pallas kernels: 5.01 us -> 3.79 us  [new_residual(): pl.pallas_call(residual_kernel, out_shape=(jax.ShapeDtypeStruct((1, ROWS,...]
where the time goes in v4:
time: 55.9 us; the launch traced here: 55.7 us
  blocking collectives  34.8 us (62%)
  Pallas kernels  12.2 us (22%)
  starting transfers between devices  4.92 us (9%)
  waiting for transfers between devices  3.16 us (6%)
  between operations  0.65 us (1%)
    all_to_all x1, blocking collectives, body(): arrived = lax.all_to_all(both, 'dp', 0, 0, tiled=True)  21 us
    all_to_all x1, blocking collectives, body(): mine = lax.all_to_all(spread(arrived), 'dp', 0, 0, tiled=True)  13.8 us
    pallas_call x1, Pallas kernels, project(): pl.pallas_call(project_kernel, out_shape=(pltpu.VMEM((ROWS, LANES), BF16)...  6.66 us
    pallas_call x1, Pallas kernels, new_residual(): pl.pallas_call(residual_kernel, out_shape=(jax.ShapeDtypeStruct((1, ROWS,...  3.79 us
    ppermute x1, starting transfers between devices, body(): other = lax.ppermute(mine, 'grp', SWAP)  3.06 us
    pallas_call x1, Pallas kernels, orthonormal_bases(): pl.pallas_call(basis_kernel, out_shape=(jax.ShapeDtypeStruct((len(SIZES),...  1.63 us
    ppermute x1, starting transfers between devices, body(): both = keep + lax.ppermute(send, 'grp', SWAP)  1.46 us
    ppermute x1, waiting for transfers between devices, body(): both = keep + lax.ppermute(send, 'grp', SWAP)  1.16 us
  transfers between devices with their start and end apart: 3, of which 3 were waited for; matrix products, arithmetic and copies ran while one was open for 0% of the time, Pallas kernels for 0%

profile of v4, /device:TPU:1, one launch (start us, length us, event | category | flops | bytes accessed | tf_op | source)
XLA Modules:
  0.0 55.7 jit_solution(15159797192543316020)
XLA Ops:
  0.6 6.7 %project.1 = (bf16[32768,128]{1,0:T(8,128)(2,1)S(1)}, f32[64,4,256]{2,1,0:T(4,128)S(1)}, f32[64,4,256]{2,1,0:T(4,128)S(1)}) custom-call(bf16[1,32768,128]{2,1,0:T(8,128)(2,1)} %grad.1, bf16[1,32768,128]{2,1,0:T(8,128)(2,1)} %residual.1, f32[5,4,128]{2,1,0:T(4,128)} %q_hbm.1), custom_call_target="tpu_custom_call" | custom-call | tf_op jit(solution)/shard_map/project/pallas_call | solution.py:100
  7.3 1.5 %collective-permute-start = (f32[64,4,256]{2,1,0:T(4,128)S(1)}, f32[64,4,256]{2,1,0:T(4,128)S(1)}, u32[]{:S(2)}, u32[]{:S(2)}) collective-permute-start(f32[64,4,256]{2,1,0:T(4,128)S(1)} %get-tuple-element.9), channel_id=1, source_target_pairs={{0,64},{64,0},{1,65},{65,1},{2,66},{66,2},{3,67},{67,3},{4,68},{68... | collective-permute-start | bytes 786440 | tf_op jit(solution)/shard_map/ppermute | solution.py:349
  8.8 1.2 %collective-permute-done = f32[64,4,256]{2,1,0:T(4,128)S(1)} collective-permute-done((f32[64,4,256]{2,1,0:T(4,128)S(1)}, f32[64,4,256]{2,1,0:T(4,128)S(1)}, u32[]{:S(2)}, u32[]{:S(2)}) %collective-permute-start) | collective-permute-done | bytes 262176 | tf_op jit(solution)/shard_map/ppermute | solution.py:349
  9.9 0.1 add.3
  10.0 21.0 %all_to_all.10.x_ref = f32[64,4,256]{2,1,0:T(4,128)S(1)} all-to-all(f32[64,4,256]{2,1,0:T(4,128)S(1)} %add.3), channel_id=1, replica_groups=mesh['grp'=2,'dp'=64] {'dp'}, dimensions={0} | all-to-all | bytes 524288 | tf_op jit(solution)/shard_map/all_to_all | solution.py:350
  30.9 0.1 spread.1
  31.0 13.8 %all_to_all.11.mine = f32[64,4,256]{2,1,0:T(4,128)S(1)} all-to-all(f32[64,4,256]{2,1,0:T(4,128)S(1)} %spread.1), channel_id=1, replica_groups=mesh['grp'=2,'dp'=64] {'dp'}, dimensions={0} | all-to-all | bytes 524288 | tf_op jit(solution)/shard_map/all_to_all | solution.py:351
  44.8 3.1 %collective-permute-start.1 = (f32[64,4,256]{2,1,0:T(4,128)S(1)}, f32[64,4,256]{2,1,0:T(4,128)S(1)}, u32[]{:S(2)}, u32[]{:S(2)}) collective-permute-start(f32[64,4,256]{2,1,0:T(4,128)S(1)} %all_to_all.11.mine), channel_id=1, source_target_pairs={{0,64},{64,0},{1,65},{65,1},{2,66},{66,2},{3,67},{67,3},{4,68},{68... | collective-permute-start | bytes 786440 | tf_op jit(solution)/shard_map/ppermute | solution.py:352
  47.9 1.2 %collective-permute-done.1.other.other_half = f32[64,4,256]{2,1,0:T(4,128)S(1)} collective-permute-done((f32[64,4,256]{2,1,0:T(4,128)S(1)}, f32[64,4,256]{2,1,0:T(4,128)S(1)}, u32[]{:S(2)}, u32[]{:S(2)}) %collective-permute-start.1) | collective-permute-done | bytes 262176 | tf_op jit(solution)/shard_map/ppermute | solution.py:352
  49.1 1.6 %bases.1 = (f32[5,4,128]{2,1,0:T(4,128)S(1)}, bf16[8,128,128]{2,1,0:T(8,128)(2,1)S(1)}) custom-call(f32[64,4,256]{2,1,0:T(4,128)S(1)} %all_to_all.11.mine, f32[64,4,256]{2,1,0:T(4,128)S(1)} %collective-permute-done.1.other.other_half, bf16[32768,128]{1,0:T(8,128)(2,1)S(1)} %get-tuple-element.10.comp), custom_call_target="tpu_custom_call" | custom-call | tf_op jit(solution)/shard_map/bases/pallas_call | solution.py:226
  50.7 0.4 collective-permute-start.2
  51.1 0.8 %collective-permute-done.2.q_other = f32[5,4,128]{2,1,0:T(4,128)S(1)} collective-permute-done((f32[5,4,128]{2,1,0:T(4,128)S(1)}, f32[5,4,128]{2,1,0:T(4,128)S(1)}, u32[]{:S(2)}, u32[]{:S(2)}) %collective-permute-start.2) | collective-permute-done | bytes 10272 | tf_op jit(solution)/shard_map/ppermute | solution.py:354
  51.9 3.8 %new_residual.1 = (bf16[1,32768,128]{2,1,0:T(8,128)(2,1)}, f32[5,4,128]{2,1,0:T(4,128)}, f32[1,4,14336]{2,1,0:T(4,128)}) custom-call(s32[5]{0:T(128)} %owner_hbm.1, f32[5,4,128]{2,1,0:T(4,128)S(1)} %get-tuple-element.11.q_mine, f32[5,4,128]{2,1,0:T(4,128)S(1)} %collective-permute-done.2.q_other, bf16[8,128,128]{2,1,0:T(8,128)(2,1)S(1)} %get-tuple-element.12.turned, ...), custom_call_target="tpu_custom_call" | custom-call | tf_op jit(solution)/shard_map/new_residual/pallas_call | solution.py:322
Async XLA Ops:
  7.3 2.6 %collective-permute-start = (f32[64,4,256]{2,1,0:T(4,128)S(1)}, f32[64,4,256]{2,1,0:T(4,128)S(1)}, u32[]{:S(2)}, u32[]{:S(2)}) collective-permute-start(f32[64,4,256]{2,1,0:T(4,128)S(1)} %get-tuple-element.9), channel_id=1, source_target_pairs={{0,64},{64,0},{1,65},{65,1},{2,66},{66,2},{3,67},{67,3},{4,68},{68... | collective-permute-start | bytes 786440 | tf_op jit(solution)/shard_map/ppermute | solution.py:349
  44.8 4.2 %collective-permute-start.1 = (f32[64,4,256]{2,1,0:T(4,128)S(1)}, f32[64,4,256]{2,1,0:T(4,128)S(1)}, u32[]{:S(2)}, u32[]{:S(2)}) collective-permute-start(f32[64,4,256]{2,1,0:T(4,128)S(1)} %all_to_all.11.mine), channel_id=1, source_target_pairs={{0,64},{64,0},{1,65},{65,1},{2,66},{66,2},{3,67},{67,3},{4,68},{68... | collective-permute-start | bytes 786440 | tf_op jit(solution)/shard_map/ppermute | solution.py:352
  50.7 1.2 %collective-permute-start.2 = (f32[5,4,128]{2,1,0:T(4,128)S(1)}, f32[5,4,128]{2,1,0:T(4,128)S(1)}, u32[]{:S(2)}, u32[]{:S(2)}) collective-permute-start(f32[5,4,128]{2,1,0:T(4,128)S(1)} %get-tuple-element.11.q_mine), channel_id=1, source_target_pairs={{0,64},{64,0},{1,65},{65,1},{2,66},{66,2},{3,67},{67,3},{4,68},{68... | collective-permute-start | bytes 30728 | tf_op jit(solution)/shard_map/ppermute | solution.py:354

commit v5 on v3

--- a/solution.py
+++ b/solution.py
@@ -36,15 +36,18 @@
 
 
 VM = pl.BlockSpec(memory_space=pltpu.VMEM)
-SM = pl.BlockSpec(memory_space=pltpu.SMEM)
 HB = pl.BlockSpec(memory_space=pltpu.HBM)
 
 
-CHUNKS = (16, 16, 16, 8, 4, 4)
+CHUNKS = (8, 16, 24, 8, 4, 4)
 DEPTH = 3
 
 
-def project_kernel(grad, residual, q_hbm, comp_ref, keep_ref, send_ref, gbuf, rbuf, q_ref, lhs, sems, q_sem):
+def project_kernel(
+    grad, residual, q_hbm, owner_hbm,
+    comp_ref, keep_ref, send_ref, flags_ref,
+    gbuf, rbuf, q_ref, lhs, owner, sems, q_sem, owner_sem,
+):
     firsts = [sum(CHUNKS[:c]) for c in range(len(CHUNKS))]
 
     def copies(c):
@@ -56,6 +59,8 @@
 
     q_copy = pltpu.make_async_copy(q_hbm, q_ref, q_sem)
     q_copy.start()
+    owner_copy = pltpu.make_async_copy(owner_hbm, owner, owner_sem)
+    owner_copy.start()
     for c in range(DEPTH):
         for copy in copies(c):
             copy.start()
@@ -71,6 +76,10 @@
             [jnp.concatenate([zero, q], 1), jnp.concatenate([q, zero], 1)], 0
         )
         lhs[layer] = jnp.where(own == 0, straight, crossed)
+    owner_copy.wait()
+    place = lax.axis_index("dp")
+    for layer in range(len(SIZES)):
+        flags_ref[layer] = jnp.full((4, HALF), jnp.where(owner[layer] == place, 1.0, 0.0), F32)
 
     layers = tile_layers()
     for c, count in enumerate(CHUNKS):
@@ -96,24 +105,31 @@
             send_ref[t] = out[4:]
 
 
-def project(grad, residual, q_prev):
+def project(grad, residual, q_prev, owner_table):
     share = jax.ShapeDtypeStruct((TILES, 4, HALF), F32)
     return pl.pallas_call(
         project_kernel,
-        out_shape=(pltpu.VMEM((ROWS, LANES), BF16), share, share),
-        in_specs=[HB, HB, HB],
-        out_specs=(VM, VM, VM),
+        out_shape=(
+            pltpu.VMEM((ROWS, LANES), BF16),
+            share,
+            share,
+            pltpu.VMEM((len(SIZES), 4, HALF), F32),
+        ),
+        in_specs=[HB, HB, HB, HB],
+        out_specs=(VM, VM, VM, VM),
         scratch_shapes=[
             pltpu.VMEM((ROWS, LANES), BF16),
             pltpu.VMEM((ROWS, LANES), BF16),
             pltpu.VMEM((len(SIZES), 4, LANES), F32),
             pltpu.VMEM((len(SIZES), 8, 2 * LANES), F32),
+            pltpu.SMEM((len(SIZES),), jnp.int32),
             pltpu.SemaphoreType.DMA((2, len(CHUNKS))),
+            pltpu.SemaphoreType.DMA,
             pltpu.SemaphoreType.DMA,
         ],
         compiler_params=pltpu.CompilerParams(vmem_limit_bytes=30 * MIB),
         name="project",
-    )(*(pltpu.with_memory_space_constraint(x, pltpu.HBM) for x in (grad, residual, q_prev)))
+    )(*(pltpu.with_memory_space_constraint(x, pltpu.HBM) for x in (grad, residual, q_prev, owner_table)))
 
 
 def spread_kernel(x_ref, o_ref):
@@ -177,36 +193,37 @@
         columns.append(
             [
                 jnp.broadcast_to(packed[:, layer : layer + 1], (8, 2 * LANES))
-                for layer in range(len(SIZES))
+                for layer in range(len(grams))
             ]
         )
     return columns
 
 
-def basis_kernel(mine, other, comp, q_ref, turned_ref, joined, stacked):
+EARLY, LATE = (0,), (4, 3, 1, 2)
+
+
+def basis_kernel(mine, other, comp, q_ref, stacked, joined):
     own = lax.axis_index("grp")
     counts = [rows // TILE for rows in SIZES]
     starts = layer_starts()
 
-    grams = []
-    for layer, count in enumerate(counts):
+    def gram(layer):
         sums = [None] * 4
-        for t in range(starts[layer], starts[layer] + count):
+        for t in range(starts[layer], starts[layer] + counts[layer]):
             v = jnp.concatenate([mine[t], other[t]], 0)
             joined[t] = v
             for k in range(4):
                 term = v * (pltpu.roll(v, k, 0) if k else v)
                 sums[k] = term if sums[k] is None else sums[k] + term
-        grams.append(sums)
-    columns = coefficients(grams)
-
-    for layer, count in enumerate(counts):
+        return sums
+
+    def apply(layer, columns):
         total = None
-        for t in range(starts[layer], starts[layer] + count):
+        for t in range(starts[layer], starts[layer] + counts[layer]):
             v = joined[t]
-            basis = v * columns[0][layer]
+            basis = v * columns[0]
             for k in range(1, 4):
-                basis = basis + pltpu.roll(v, k, 0) * columns[k][layer]
+                basis = basis + pltpu.roll(v, k, 0) * columns[k]
             rounded = basis.astype(BF16)
             back = rounded.astype(F32)
             at = (t % GROUP) * 16
@@ -219,8 +236,14 @@
             )
             total = part if total is None else total + part
         q_ref[layer] = total[:4, :LANES] + total[4:, LANES:]
-    for n in range(TILES // GROUP):
-        turned_ref[n] = stacked[n].T.astype(BF16)
+
+    early = coefficients([gram(layer) for layer in EARLY])
+    late_grams = [gram(layer) for layer in LATE]
+    for i, layer in enumerate(EARLY):
+        apply(layer, [column[i] for column in early])
+    late = coefficients(late_grams)
+    for i, layer in enumerate(LATE):
+        apply(layer, [column[i] for column in late])
 
 
 def orthonormal_bases(mine, other, comp):
@@ -228,48 +251,58 @@
         basis_kernel,
         out_shape=(
             jax.ShapeDtypeStruct((len(SIZES), 4, LANES), F32),
-            pltpu.VMEM((TILES // GROUP, LANES, LANES), BF16),
+            pltpu.VMEM((TILES // GROUP, LANES, LANES), F32),
         ),
         in_specs=[VM, VM, VM],
         out_specs=(VM, VM),
-        scratch_shapes=[
-            pltpu.VMEM((TILES, 8, HALF), F32),
-            pltpu.VMEM((TILES // GROUP, LANES, LANES), F32),
-        ],
+        scratch_shapes=[pltpu.VMEM((TILES, 8, HALF), F32)],
         compiler_params=pltpu.CompilerParams(vmem_limit_bytes=16 * MIB),
         name="bases",
     )(mine, other, comp)
 
 
-PIECE = 4
-PIECES = TILES // PIECE
-
-
-def residual_kernel(
-    owner, q_mine, q_other, turned, comp, mine, other_half, out_hbm, q_ref, owned_hbm, weights, obuf, owned, sems
-):
-    own, place = lax.axis_index("grp"), lax.axis_index("dp")
-    owned_copy = pltpu.make_async_copy(owned, owned_hbm, sems.at[PIECES])
-
-    def write_owned():
-        owned[...] = jnp.zeros_like(owned)
-        for layer, first in enumerate(layer_starts()):
-
-            @pl.when(owner[layer] == place)
-            def _():
-                def step(k, _):
-                    at = pl.multiple_of(k * TILE + own * HALF, HALF)
-                    owned[0, :, pl.ds(at, HALF)] = mine[first + k]
-                    at = pl.multiple_of(k * TILE + (1 - own) * HALF, HALF)
-                    owned[0, :, pl.ds(at, HALF)] = other_half[first + k]
-
-                lax.fori_loop(0, SIZES[layer] // TILE, step, None)
-
-        owned_copy.start()
-
+def aside_kernel(flags, mine, other, stacked, turned_ref, owned_ref):
+    own = lax.axis_index("grp")
+    for n in range(TILES // GROUP):
+        turned_ref[n] = stacked[n].T.astype(BF16)
+    starts = layer_starts()
+    counts = [rows // TILE for rows in SIZES]
+    held = [flags[layer] > 0.5 for layer in range(len(SIZES))]
+    for k in range(max(counts)):
+        for ref, which in ((mine, own), (other, 1 - own)):
+            value = jnp.zeros((4, HALF), F32)
+            for layer, first in enumerate(starts):
+                if k < counts[layer]:
+                    value = jnp.where(held[layer], ref[first + k], value)
+            owned_ref[0, :, pl.ds(pl.multiple_of(k * TILE + which * HALF, HALF), HALF)] = value
+
+
+def aside(flags, mine, other, stacked):
+    return pl.pallas_call(
+        aside_kernel,
+        out_shape=(
+            pltpu.VMEM((TILES // GROUP, LANES, LANES), BF16),
+            pltpu.VMEM((1, 4, max(SIZES)), F32),
+        ),
+        in_specs=[VM, VM, VM, VM],
+        out_specs=(VM, VM),
+        compiler_params=pltpu.CompilerParams(vmem_limit_bytes=4 * MIB),
+        cost_estimate=pl.CostEstimate(flops=2_000_000, bytes_accessed=1_000_000, transcendentals=0),
+        name="aside",
+    )(flags, mine, other, stacked)
+
+
+PIECES = (4,) * 16
+
+
+def residual_kernel(q_mine, q_other, turned, comp, out_hbm, q_hbm, weights, obuf, q_ref, sems):
+    own = lax.axis_index("grp")
+    q_copy = pltpu.make_async_copy(q_ref, q_hbm, sems.at[len(PIECES)])
+    ends = [sum(PIECES[: n + 1]) for n in range(len(PIECES))]
     layers = tile_layers()
     q_new = (q_mine[...] + q_other[...]) * 0.5
     q_ref[...] = q_new
+    q_copy.start()
     rounded = q_new.astype(BF16).astype(F32)
     zero = jnp.zeros((4, LANES), F32)
     for layer in range(len(SIZES)):
@@ -280,7 +313,7 @@
         weights[layer, 1] = jnp.concatenate([none, rows[0], none, rows[1]], 0)
 
     def copy(n):
-        rows = pl.ds(n * PIECE * TILE, PIECE * TILE)
+        rows = pl.ds((ends[n] - PIECES[n]) * TILE, PIECES[n] * TILE)
         return pltpu.make_async_copy(obuf.at[rows], out_hbm.at[0, rows], sems.at[n])
 
     for n in range(TILES // GROUP):
@@ -302,45 +335,44 @@
                     obuf[rows] = (
                         comp[rows].astype(F32) - update[:, h * LANES : (h + 1) * LANES]
                     ).astype(BF16)
-            if t % PIECE == PIECE - 1:
-                copy(t // PIECE).start()
-        if n == 1:
-            write_owned()
-    owned_copy.wait()
-    for n in range(PIECES):
+            if t + 1 in ends:
+                copy(ends.index(t + 1)).start()
+    q_copy.wait()
+    for n in range(len(PIECES)):
         copy(n).wait()
 
 
-def new_residual(owner_table, q_mine, q_other, turned, comp, mine, other):
+def new_residual(q_mine, q_other, turned, comp):
     return pl.pallas_call(
         residual_kernel,
         out_shape=(
             jax.ShapeDtypeStruct((1, ROWS, LANES), BF16),
             jax.ShapeDtypeStruct((len(SIZES), 4, LANES), F32),
-            jax.ShapeDtypeStruct((1, 4, max(SIZES)), F32),
         ),
-        in_specs=[SM, VM, VM, VM, VM, VM, VM],
-        out_specs=(HB, VM, HB),
+        in_specs=[VM, VM, VM, VM],
+        out_specs=(HB, HB),
         scratch_shapes=[
             pltpu.VMEM((len(SIZES), 2, 16, 2 * LANES), F32),
             pltpu.VMEM((ROWS, LANES), BF16),
-            pltpu.VMEM((1, 4, max(SIZES)), F32),
-            pltpu.SemaphoreType.DMA((PIECES + 1,)),
+            pltpu.VMEM((len(SIZES), 4, LANES), F32),
+            pltpu.SemaphoreType.DMA((len(PIECES) + 1,)),
         ],
         compiler_params=pltpu.CompilerParams(vmem_limit_bytes=24 * MIB),
         name="new_residual",
-    )(owner_table, q_mine, q_other, turned, comp, mine, other)
+    )(q_mine, q_other, turned, comp)
 
 
 def body(grad, residual, q_prev, owner_table):
-    comp, keep, send = project(grad, residual, q_prev)
+    comp, keep, send, flags = project(grad, residual, q_prev, owner_table)
     both = keep + lax.ppermute(send, "grp", SWAP)
     arrived = lax.all_to_all(both, "dp", 0, 0, tiled=True)
     mine = lax.all_to_all(spread(arrived), "dp", 0, 0, tiled=True)
     other = lax.ppermute(mine, "grp", SWAP)
-    q_part, turned = orthonormal_bases(mine, other, comp)
+    q_part, stacked = orthonormal_bases(mine, other, comp)
     q_there = lax.ppermute(q_part, "grp", SWAP)
-    return new_residual(owner_table, q_part, q_there, turned, comp, mine, other)
+    turned, owned = aside(flags, mine, other, stacked)
+    out, q_new = new_residual(q_part, q_there, turned, comp)
+    return out, q_new, owned
 
 
 def solution(mesh):

time: 57.3 us -> 55.8 us (0.974)
  Pallas kernels: 13.6 us -> 12.1 us
  waiting for transfers between devices: 3.16 us -> 2.33 us
  local copies, waits for them, and re-layouts: 0.01 us -> 0.69 us
    pallas_call x1, Pallas kernels: 5.01 us -> 3.7 us  [new_residual(): pl.pallas_call(residual_kernel, out_shape=(jax.ShapeDtypeStruct((1, ROWS,...]
    ppermute x1, waiting for transfers between devices: 0.83 us -> 0.01 us  [body(): q_there = lax.ppermute(q_part, 'grp', SWAP)]
    unnamed x2 -> x1, local copies, waits for them, and re-layouts: 0.01 us -> 0.69 us
  transfers between devices with their start and end apart: 3 -> 3, of which waited for: 3 -> 2; matrix products, arithmetic and copies ran while one was open for 0% -> 1% of each run, Pallas kernels for 0% -> 0%
where the time goes in v5:
time: 55.8 us; the launch traced here: 55.6 us
  blocking collectives  34.8 us (62%)
  Pallas kernels  12.1 us (22%)
  starting transfers between devices  4.95 us (9%)
  waiting for transfers between devices  2.33 us (4%)
  local copies, waits for them, and re-layouts  0.69 us (1%)
  between operations  0.66 us (1%)
    all_to_all x1, blocking collectives, body(): arrived = lax.all_to_all(both, 'dp', 0, 0, tiled=True)  21 us
    all_to_all x1, blocking collectives, body(): mine = lax.all_to_all(spread(arrived), 'dp', 0, 0, tiled=True)  13.8 us
    pallas_call x1, Pallas kernels, project(): pl.pallas_call(project_kernel, out_shape=(pltpu.VMEM((ROWS, LANES), BF16)...  6.72 us
    pallas_call x1, Pallas kernels, new_residual(): pl.pallas_call(residual_kernel, out_shape=(jax.ShapeDtypeStruct((1, ROWS,...  3.7 us
    ppermute x1, starting transfers between devices, body(): other = lax.ppermute(mine, 'grp', SWAP)  3.06 us
    pallas_call x1, Pallas kernels, orthonormal_bases(): pl.pallas_call(basis_kernel, out_shape=(jax.ShapeDtypeStruct((len(SIZES),...  1.5 us
    ppermute x1, starting transfers between devices, body(): both = keep + lax.ppermute(send, 'grp', SWAP)  1.46 us
    ppermute x1, waiting for transfers between devices, body(): both = keep + lax.ppermute(send, 'grp', SWAP)  1.16 us
  transfers between devices with their start and end apart: 3, of which 2 were waited for; matrix products, arithmetic and copies ran while one was open for 1% of the time, Pallas kernels for 0%

profile of v5, /device:TPU:1, one launch (start us, length us, event | category | flops | bytes accessed | tf_op | source)
XLA Modules:
  0.0 55.6 jit_solution(12623721139262121609)
XLA Ops:
  0.6 6.7 %project.1 = (bf16[32768,128]{1,0:T(8,128)(2,1)S(1)}, f32[64,4,256]{2,1,0:T(4,128)S(1)}, f32[64,4,256]{2,1,0:T(4,128)S(1)}, f32[5,4,256]{2,1,0:T(4,128)S(1)}) custom-call(bf16[1,32768,128]{2,1,0:T(8,128)(2,1)} %grad.1, bf16[1,32768,128]{2,1,0:T(8,128)(2,1)} %residual.1, f32[5,4,128]{2,1,0:T(4,128)} %q_hbm.1, s32[5]{0:T(128)} %owner_hbm.1), custom_call_target="tpu_custom_call" | custom-call | tf_op jit(solution)/shard_map/project/pallas_call | solution.py:110
  7.4 1.5 %collective-permute-start = (f32[64,4,256]{2,1,0:T(4,128)S(1)}, f32[64,4,256]{2,1,0:T(4,128)S(1)}, u32[]{:S(2)}, u32[]{:S(2)}) collective-permute-start(f32[64,4,256]{2,1,0:T(4,128)S(1)} %get-tuple-element.14), channel_id=1, source_target_pairs={{0,64},{64,0},{1,65},{65,1},{2,66},{66,2},{3,67},{67,3},{4,68},{68... | collective-permute-start | bytes 786440 | tf_op jit(solution)/shard_map/ppermute | solution.py:367
  8.8 1.2 %collective-permute-done = f32[64,4,256]{2,1,0:T(4,128)S(1)} collective-permute-done((f32[64,4,256]{2,1,0:T(4,128)S(1)}, f32[64,4,256]{2,1,0:T(4,128)S(1)}, u32[]{:S(2)}, u32[]{:S(2)}) %collective-permute-start) | collective-permute-done | bytes 262176 | tf_op jit(solution)/shard_map/ppermute | solution.py:367
  10.0 0.1 add.3
  10.1 21.0 %all_to_all.10.x_ref = f32[64,4,256]{2,1,0:T(4,128)S(1)} all-to-all(f32[64,4,256]{2,1,0:T(4,128)S(1)} %add.3), channel_id=1, replica_groups=mesh['grp'=2,'dp'=64] {'dp'}, dimensions={0} | all-to-all | bytes 524288 | tf_op jit(solution)/shard_map/all_to_all | solution.py:368
  31.0 0.1 spread.1
  31.1 13.8 %all_to_all.11.mine = f32[64,4,256]{2,1,0:T(4,128)S(1)} all-to-all(f32[64,4,256]{2,1,0:T(4,128)S(1)} %spread.1), channel_id=1, replica_groups=mesh['grp'=2,'dp'=64] {'dp'}, dimensions={0} | all-to-all | bytes 524288 | tf_op jit(solution)/shard_map/all_to_all | solution.py:369
  44.9 3.1 %collective-permute-start.1 = (f32[64,4,256]{2,1,0:T(4,128)S(1)}, f32[64,4,256]{2,1,0:T(4,128)S(1)}, u32[]{:S(2)}, u32[]{:S(2)}) collective-permute-start(f32[64,4,256]{2,1,0:T(4,128)S(1)} %all_to_all.11.mine), channel_id=1, source_target_pairs={{0,64},{64,0},{1,65},{65,1},{2,66},{66,2},{3,67},{67,3},{4,68},{68... | collective-permute-start | bytes 786440 | tf_op jit(solution)/shard_map/ppermute | solution.py:370
  48.0 1.2 %collective-permute-done.1.other = f32[64,4,256]{2,1,0:T(4,128)S(1)} collective-permute-done((f32[64,4,256]{2,1,0:T(4,128)S(1)}, f32[64,4,256]{2,1,0:T(4,128)S(1)}, u32[]{:S(2)}, u32[]{:S(2)}) %collective-permute-start.1) | collective-permute-done | bytes 262176 | tf_op jit(solution)/shard_map/ppermute | solution.py:370
  49.1 1.5 %bases.1 = (f32[5,4,128]{2,1,0:T(4,128)S(1)}, f32[8,128,128]{2,1,0:T(8,128)S(1)}) custom-call(f32[64,4,256]{2,1,0:T(4,128)S(1)} %all_to_all.11.mine, f32[64,4,256]{2,1,0:T(4,128)S(1)} %collective-permute-done.1.other, bf16[32768,128]{1,0:T(8,128)(2,1)S(1)} %get-tuple-element.15.comp), custom_call_target="tpu_custom_call" | custom-call | tf_op jit(solution)/shard_map/bases/pallas_call | solution.py:250
  50.6 0.4 collective-permute-start.2
  51.0 0.1 aside.1
  51.2 0.7 %copy.7 = f32[1,4,14336]{2,1,0:T(4,128)} copy(f32[1,4,14336]{2,1,0:T(4,128)S(1)} %get-tuple-element.25) | data formatting | bytes 458752
  51.9 0.0 collective-permute-done.2.q_other
  51.9 3.7 %new_residual.1 = (bf16[1,32768,128]{2,1,0:T(8,128)(2,1)}, f32[5,4,128]{2,1,0:T(4,128)}) custom-call(f32[5,4,128]{2,1,0:T(4,128)S(1)} %get-tuple-element.16.q_mine, f32[5,4,128]{2,1,0:T(4,128)S(1)} %collective-permute-done.2.q_other, bf16[8,128,128]{2,1,0:T(8,128)(2,1)S(1)} %get-tuple-element.19.turned, bf16[32768,128]{1,0:T(8,128)(2,1)S(1)} %get-tuple-element.15.comp), custom_call_target="tpu_custom_call" | custom-call | tf_op jit(solution)/shard_map/new_residual/pallas_call | solution.py:346
Async XLA Ops:
  7.4 2.6 %collective-permute-start = (f32[64,4,256]{2,1,0:T(4,128)S(1)}, f32[64,4,256]{2,1,0:T(4,128)S(1)}, u32[]{:S(2)}, u32[]{:S(2)}) collective-permute-start(f32[64,4,256]{2,1,0:T(4,128)S(1)} %get-tuple-element.14), channel_id=1, source_target_pairs={{0,64},{64,0},{1,65},{65,1},{2,66},{66,2},{3,67},{67,3},{4,68},{68... | collective-permute-start | bytes 786440 | tf_op jit(solution)/shard_map/ppermute | solution.py:367
  44.9 4.2 %collective-permute-start.1 = (f32[64,4,256]{2,1,0:T(4,128)S(1)}, f32[64,4,256]{2,1,0:T(4,128)S(1)}, u32[]{:S(2)}, u32[]{:S(2)}) collective-permute-start(f32[64,4,256]{2,1,0:T(4,128)S(1)} %all_to_all.11.mine), channel_id=1, source_target_pairs={{0,64},{64,0},{1,65},{65,1},{2,66},{66,2},{3,67},{67,3},{4,68},{68... | collective-permute-start | bytes 786440 | tf_op jit(solution)/shard_map/ppermute | solution.py:370
  50.6 1.3 %collective-permute-start.2 = (f32[5,4,128]{2,1,0:T(4,128)S(1)}, f32[5,4,128]{2,1,0:T(4,128)S(1)}, u32[]{:S(2)}, u32[]{:S(2)}) collective-permute-start(f32[5,4,128]{2,1,0:T(4,128)S(1)} %get-tuple-element.16.q_mine), channel_id=1, source_target_pairs={{0,64},{64,0},{1,65},{65,1},{2,66},{66,2},{3,67},{67,3},{4,68},{68... | collective-permute-start | bytes 30728 | tf_op jit(solution)/shard_map/ppermute | solution.py:372

commit v6 on v5

--- a/solution.py
+++ b/solution.py
@@ -39,7 +39,7 @@
 HB = pl.BlockSpec(memory_space=pltpu.HBM)
 
 
-CHUNKS = (8, 16, 24, 8, 4, 4)
+CHUNKS = (6, 14, 22, 12, 6, 4)
 DEPTH = 3
 
 
@@ -76,10 +76,6 @@
             [jnp.concatenate([zero, q], 1), jnp.concatenate([q, zero], 1)], 0
         )
         lhs[layer] = jnp.where(own == 0, straight, crossed)
-    owner_copy.wait()
-    place = lax.axis_index("dp")
-    for layer in range(len(SIZES)):
-        flags_ref[layer] = jnp.full((4, HALF), jnp.where(owner[layer] == place, 1.0, 0.0), F32)
 
     layers = tile_layers()
     for c, count in enumerate(CHUNKS):
@@ -88,6 +84,12 @@
         if c + DEPTH < len(CHUNKS):
             for copy in copies(c + DEPTH):
                 copy.start()
+        if c == 1:
+            owner_copy.wait()
+            place = lax.axis_index("dp")
+            for layer in range(len(SIZES)):
+                held = jnp.where(owner[layer] == place, 1.0, 0.0)
+                flags_ref[layer] = jnp.full((4, HALF), held, F32)
         for t in range(firsts[c], firsts[c] + count):
             halves = []
             for h in range(2):
@@ -295,8 +297,12 @@
 PIECES = (4,) * 16
 
 
-def residual_kernel(q_mine, q_other, turned, comp, out_hbm, q_hbm, weights, obuf, q_ref, sems):
+def residual_kernel(
+    q_mine, q_other, turned, comp, owned, out_hbm, q_hbm, owned_hbm, weights, obuf, q_ref, sems
+):
     own = lax.axis_index("grp")
+    owned_copy = pltpu.make_async_copy(owned, owned_hbm, sems.at[len(PIECES) + 1])
+    owned_copy.start()
     q_copy = pltpu.make_async_copy(q_ref, q_hbm, sems.at[len(PIECES)])
     ends = [sum(PIECES[: n + 1]) for n in range(len(PIECES))]
     layers = tile_layers()
@@ -337,29 +343,31 @@
                     ).astype(BF16)
             if t + 1 in ends:
                 copy(ends.index(t + 1)).start()
+    owned_copy.wait()
     q_copy.wait()
     for n in range(len(PIECES)):
         copy(n).wait()
 
 
-def new_residual(q_mine, q_other, turned, comp):
+def new_residual(q_mine, q_other, turned, comp, owned):
     return pl.pallas_call(
         residual_kernel,
         out_shape=(
             jax.ShapeDtypeStruct((1, ROWS, LANES), BF16),
             jax.ShapeDtypeStruct((len(SIZES), 4, LANES), F32),
+            jax.ShapeDtypeStruct((1, 4, max(SIZES)), F32),
         ),
-        in_specs=[VM, VM, VM, VM],
-        out_specs=(HB, HB),
+        in_specs=[VM, VM, VM, VM, VM],
+        out_specs=(HB, HB, HB),
         scratch_shapes=[
             pltpu.VMEM((len(SIZES), 2, 16, 2 * LANES), F32),
             pltpu.VMEM((ROWS, LANES), BF16),
             pltpu.VMEM((len(SIZES), 4, LANES), F32),
-            pltpu.SemaphoreType.DMA((len(PIECES) + 1,)),
+            pltpu.SemaphoreType.DMA((len(PIECES) + 2,)),
         ],
         compiler_params=pltpu.CompilerParams(vmem_limit_bytes=24 * MIB),
         name="new_residual",
-    )(q_mine, q_other, turned, comp)
+    )(q_mine, q_other, turned, comp, owned)
 
 
 def body(grad, residual, q_prev, owner_table):
@@ -371,8 +379,7 @@
     q_part, stacked = orthonormal_bases(mine, other, comp)
     q_there = lax.ppermute(q_part, "grp", SWAP)
     turned, owned = aside(flags, mine, other, stacked)
-    out, q_new = new_residual(q_part, q_there, turned, comp)
-    return out, q_new, owned
+    return new_residual(q_part, q_there, turned, comp, owned)
 
 
 def solution(mesh):

time: 55.8 us -> 55.6 us (level)
  local copies, waits for them, and re-layouts: 0.69 us -> 0 us
  waiting for transfers between devices: 2.33 us -> 3.01 us
    unnamed x1 -> x0, local copies, waits for them, and re-layouts: 0.69 us -> none
    ppermute x1, waiting for transfers between devices: 0.01 us -> 0.69 us  [body(): q_there = lax.ppermute(q_part, 'grp', SWAP)]
  transfers between devices with their start and end apart: 3 -> 3, of which waited for: 2 -> 3; matrix products, arithmetic and copies ran while one was open for 1% -> 0% of each run, Pallas kernels for 0% -> 0%
where the time goes in v6:
time: 55.6 us; the launch traced here: 55.4 us
  blocking collectives  34.8 us (63%)
  Pallas kernels  12 us (22%)
  starting transfers between devices  4.95 us (9%)
  waiting for transfers between devices  3.01 us (5%)
  between operations  0.66 us (1%)
    all_to_all x1, blocking collectives, body(): arrived = lax.all_to_all(both, 'dp', 0, 0, tiled=True)  21 us
    all_to_all x1, blocking collectives, body(): mine = lax.all_to_all(spread(arrived), 'dp', 0, 0, tiled=True)  13.8 us
    pallas_call x1, Pallas kernels, project(): pl.pallas_call(project_kernel, out_shape=(pltpu.VMEM((ROWS, LANES), BF16)...  6.56 us
    pallas_call x1, Pallas kernels, new_residual(): pl.pallas_call(residual_kernel, out_shape=(jax.ShapeDtypeStruct((1, ROWS,...  3.71 us
    ppermute x1, starting transfers between devices, body(): other = lax.ppermute(mine, 'grp', SWAP)  3.06 us
    pallas_call x1, Pallas kernels, orthonormal_bases(): pl.pallas_call(basis_kernel, out_shape=(jax.ShapeDtypeStruct((len(SIZES),...  1.5 us
    ppermute x1, starting transfers between devices, body(): both = keep + lax.ppermute(send, 'grp', SWAP)  1.46 us
    ppermute x1, waiting for transfers between devices, body(): both = keep + lax.ppermute(send, 'grp', SWAP)  1.16 us
  transfers between devices with their start and end apart: 3, of which 3 were waited for; matrix products, arithmetic and copies ran while one was open for 0% of the time, Pallas kernels for 0%

profile of v6, /device:TPU:1, one launch (start us, length us, event | category | flops | bytes accessed | tf_op | source)
XLA Modules:
  0.0 55.4 jit_solution(18118530974782815315)
XLA Ops:
  0.6 6.6 %project.1 = (bf16[32768,128]{1,0:T(8,128)(2,1)S(1)}, f32[64,4,256]{2,1,0:T(4,128)S(1)}, f32[64,4,256]{2,1,0:T(4,128)S(1)}, f32[5,4,256]{2,1,0:T(4,128)S(1)}) custom-call(bf16[1,32768,128]{2,1,0:T(8,128)(2,1)} %grad.1, bf16[1,32768,128]{2,1,0:T(8,128)(2,1)} %residual.1, f32[5,4,128]{2,1,0:T(4,128)} %q_hbm.1, s32[5]{0:T(128)} %owner_hbm.1), custom_call_target="tpu_custom_call" | custom-call | tf_op jit(solution)/shard_map/project/pallas_call | solution.py:112
  7.2 1.5 %collective-permute-start = (f32[64,4,256]{2,1,0:T(4,128)S(1)}, f32[64,4,256]{2,1,0:T(4,128)S(1)}, u32[]{:S(2)}, u32[]{:S(2)}) collective-permute-start(f32[64,4,256]{2,1,0:T(4,128)S(1)} %get-tuple-element.12), channel_id=1, source_target_pairs={{0,64},{64,0},{1,65},{65,1},{2,66},{66,2},{3,67},{67,3},{4,68},{68... | collective-permute-start | bytes 786440 | tf_op jit(solution)/shard_map/ppermute | solution.py:375
  8.7 1.2 %collective-permute-done = f32[64,4,256]{2,1,0:T(4,128)S(1)} collective-permute-done((f32[64,4,256]{2,1,0:T(4,128)S(1)}, f32[64,4,256]{2,1,0:T(4,128)S(1)}, u32[]{:S(2)}, u32[]{:S(2)}) %collective-permute-start) | collective-permute-done | bytes 262176 | tf_op jit(solution)/shard_map/ppermute | solution.py:375
  9.8 0.1 add.3
  9.9 21.0 %all_to_all.10.x_ref = f32[64,4,256]{2,1,0:T(4,128)S(1)} all-to-all(f32[64,4,256]{2,1,0:T(4,128)S(1)} %add.3), channel_id=1, replica_groups=mesh['grp'=2,'dp'=64] {'dp'}, dimensions={0} | all-to-all | bytes 524288 | tf_op jit(solution)/shard_map/all_to_all | solution.py:376
  30.8 0.1 spread.1
  30.9 13.8 %all_to_all.11.mine = f32[64,4,256]{2,1,0:T(4,128)S(1)} all-to-all(f32[64,4,256]{2,1,0:T(4,128)S(1)} %spread.1), channel_id=1, replica_groups=mesh['grp'=2,'dp'=64] {'dp'}, dimensions={0} | all-to-all | bytes 524288 | tf_op jit(solution)/shard_map/all_to_all | solution.py:377
  44.7 3.1 %collective-permute-start.1 = (f32[64,4,256]{2,1,0:T(4,128)S(1)}, f32[64,4,256]{2,1,0:T(4,128)S(1)}, u32[]{:S(2)}, u32[]{:S(2)}) collective-permute-start(f32[64,4,256]{2,1,0:T(4,128)S(1)} %all_to_all.11.mine), channel_id=1, source_target_pairs={{0,64},{64,0},{1,65},{65,1},{2,66},{66,2},{3,67},{67,3},{4,68},{68... | collective-permute-start | bytes 786440 | tf_op jit(solution)/shard_map/ppermute | solution.py:378
  47.8 1.2 %collective-permute-done.1.other = f32[64,4,256]{2,1,0:T(4,128)S(1)} collective-permute-done((f32[64,4,256]{2,1,0:T(4,128)S(1)}, f32[64,4,256]{2,1,0:T(4,128)S(1)}, u32[]{:S(2)}, u32[]{:S(2)}) %collective-permute-start.1) | collective-permute-done | bytes 262176 | tf_op jit(solution)/shard_map/ppermute | solution.py:378
  49.0 1.5 %bases.1 = (f32[5,4,128]{2,1,0:T(4,128)S(1)}, f32[8,128,128]{2,1,0:T(8,128)S(1)}) custom-call(f32[64,4,256]{2,1,0:T(4,128)S(1)} %all_to_all.11.mine, f32[64,4,256]{2,1,0:T(4,128)S(1)} %collective-permute-done.1.other, bf16[32768,128]{1,0:T(8,128)(2,1)S(1)} %get-tuple-element.13.comp), custom_call_target="tpu_custom_call" | custom-call | tf_op jit(solution)/shard_map/bases/pallas_call | solution.py:252
  50.5 0.4 collective-permute-start.2
  50.9 0.1 aside.1
  51.0 0.7 %collective-permute-done.2.q_other = f32[5,4,128]{2,1,0:T(4,128)S(1)} collective-permute-done((f32[5,4,128]{2,1,0:T(4,128)S(1)}, f32[5,4,128]{2,1,0:T(4,128)S(1)}, u32[]{:S(2)}, u32[]{:S(2)}) %collective-permute-start.2) | collective-permute-done | bytes 10272 | tf_op jit(solution)/shard_map/ppermute | solution.py:380
  51.7 3.7 %new_residual.1 = (bf16[1,32768,128]{2,1,0:T(8,128)(2,1)}, f32[5,4,128]{2,1,0:T(4,128)}, f32[1,4,14336]{2,1,0:T(4,128)}) custom-call(f32[5,4,128]{2,1,0:T(4,128)S(1)} %get-tuple-element.14.q_mine, f32[5,4,128]{2,1,0:T(4,128)S(1)} %collective-permute-done.2.q_other, bf16[8,128,128]{2,1,0:T(8,128)(2,1)S(1)} %get-tuple-element.17.turned, ...), custom_call_target="tpu_custom_call" | custom-call | tf_op jit(solution)/shard_map/new_residual/pallas_call | solution.py:353
Async XLA Ops:
  7.2 2.6 %collective-permute-start = (f32[64,4,256]{2,1,0:T(4,128)S(1)}, f32[64,4,256]{2,1,0:T(4,128)S(1)}, u32[]{:S(2)}, u32[]{:S(2)}) collective-permute-start(f32[64,4,256]{2,1,0:T(4,128)S(1)} %get-tuple-element.12), channel_id=1, source_target_pairs={{0,64},{64,0},{1,65},{65,1},{2,66},{66,2},{3,67},{67,3},{4,68},{68... | collective-permute-start | bytes 786440 | tf_op jit(solution)/shard_map/ppermute | solution.py:375
  44.7 4.2 %collective-permute-start.1 = (f32[64,4,256]{2,1,0:T(4,128)S(1)}, f32[64,4,256]{2,1,0:T(4,128)S(1)}, u32[]{:S(2)}, u32[]{:S(2)}) collective-permute-start(f32[64,4,256]{2,1,0:T(4,128)S(1)} %all_to_all.11.mine), channel_id=1, source_target_pairs={{0,64},{64,0},{1,65},{65,1},{2,66},{66,2},{3,67},{67,3},{4,68},{68... | collective-permute-start | bytes 786440 | tf_op jit(solution)/shard_map/ppermute | solution.py:378
  50.5 1.3 %collective-permute-start.2 = (f32[5,4,128]{2,1,0:T(4,128)S(1)}, f32[5,4,128]{2,1,0:T(4,128)S(1)}, u32[]{:S(2)}, u32[]{:S(2)}) collective-permute-start(f32[5,4,128]{2,1,0:T(4,128)S(1)} %get-tuple-element.14.q_mine), channel_id=1, source_target_pairs={{0,64},{64,0},{1,65},{65,1},{2,66},{66,2},{3,67},{67,3},{4,68},{68... | collective-permute-start | bytes 30728 | tf_op jit(solution)/shard_map/ppermute | solution.py:380

commit v7 on v6

--- a/solution.py
+++ b/solution.py
@@ -342,7 +342,7 @@
                         comp[rows].astype(F32) - update[:, h * LANES : (h + 1) * LANES]
                     ).astype(BF16)
             if t + 1 in ends:
-                copy(ends.index(t + 1)).start()
+                copy(ends.index(t + 1)).start(priority=ends.index(t + 1) % 2)
     owned_copy.wait()
     q_copy.wait()
     for n in range(len(PIECES)):

time: 55.6 us -> 55.6 us (level)
  no operation moved by 1% of the time
where the time goes in v7:
time: 55.6 us; the launch traced here: 55.4 us
  blocking collectives  34.8 us (63%)
  Pallas kernels  12 us (22%)
  starting transfers between devices  4.95 us (9%)
  waiting for transfers between devices  3.01 us (5%)
  between operations  0.66 us (1%)
    all_to_all x1, blocking collectives, body(): arrived = lax.all_to_all(both, 'dp', 0, 0, tiled=True)  21 us
    all_to_all x1, blocking collectives, body(): mine = lax.all_to_all(spread(arrived), 'dp', 0, 0, tiled=True)  13.8 us
    pallas_call x1, Pallas kernels, project(): pl.pallas_call(project_kernel, out_shape=(pltpu.VMEM((ROWS, LANES), BF16)...  6.56 us
    pallas_call x1, Pallas kernels, new_residual(): pl.pallas_call(residual_kernel, out_shape=(jax.ShapeDtypeStruct((1, ROWS,...  3.71 us
    ppermute x1, starting transfers between devices, body(): other = lax.ppermute(mine, 'grp', SWAP)  3.06 us
    pallas_call x1, Pallas kernels, orthonormal_bases(): pl.pallas_call(basis_kernel, out_shape=(jax.ShapeDtypeStruct((len(SIZES),...  1.5 us
    ppermute x1, starting transfers between devices, body(): both = keep + lax.ppermute(send, 'grp', SWAP)  1.46 us
    ppermute x1, waiting for transfers between devices, body(): both = keep + lax.ppermute(send, 'grp', SWAP)  1.16 us
  transfers between devices with their start and end apart: 3, of which 3 were waited for; matrix products, arithmetic and copies ran while one was open for 0% of the time, Pallas kernels for 0%

profile of v7, /device:TPU:1, one launch (start us, length us, event | category | flops | bytes accessed | tf_op | source)
XLA Modules:
  0.0 55.4 jit_solution(7678650567815848373)
XLA Ops:
  0.6 6.6 %project.1 = (bf16[32768,128]{1,0:T(8,128)(2,1)S(1)}, f32[64,4,256]{2,1,0:T(4,128)S(1)}, f32[64,4,256]{2,1,0:T(4,128)S(1)}, f32[5,4,256]{2,1,0:T(4,128)S(1)}) custom-call(bf16[1,32768,128]{2,1,0:T(8,128)(2,1)} %grad.1, bf16[1,32768,128]{2,1,0:T(8,128)(2,1)} %residual.1, f32[5,4,128]{2,1,0:T(4,128)} %q_hbm.1, s32[5]{0:T(128)} %owner_hbm.1), custom_call_target="tpu_custom_call" | custom-call | tf_op jit(solution)/shard_map/project/pallas_call | solution.py:112
  7.2 1.5 %collective-permute-start = (f32[64,4,256]{2,1,0:T(4,128)S(1)}, f32[64,4,256]{2,1,0:T(4,128)S(1)}, u32[]{:S(2)}, u32[]{:S(2)}) collective-permute-start(f32[64,4,256]{2,1,0:T(4,128)S(1)} %get-tuple-element.12), channel_id=1, source_target_pairs={{0,64},{64,0},{1,65},{65,1},{2,66},{66,2},{3,67},{67,3},{4,68},{68... | collective-permute-start | bytes 786440 | tf_op jit(solution)/shard_map/ppermute | solution.py:375
  8.7 1.2 %collective-permute-done = f32[64,4,256]{2,1,0:T(4,128)S(1)} collective-permute-done((f32[64,4,256]{2,1,0:T(4,128)S(1)}, f32[64,4,256]{2,1,0:T(4,128)S(1)}, u32[]{:S(2)}, u32[]{:S(2)}) %collective-permute-start) | collective-permute-done | bytes 262176 | tf_op jit(solution)/shard_map/ppermute | solution.py:375
  9.8 0.1 add.3
  9.9 21.0 %all_to_all.10.x_ref = f32[64,4,256]{2,1,0:T(4,128)S(1)} all-to-all(f32[64,4,256]{2,1,0:T(4,128)S(1)} %add.3), channel_id=1, replica_groups=mesh['grp'=2,'dp'=64] {'dp'}, dimensions={0} | all-to-all | bytes 524288 | tf_op jit(solution)/shard_map/all_to_all | solution.py:376
  30.8 0.1 spread.1
  30.9 13.8 %all_to_all.11.mine = f32[64,4,256]{2,1,0:T(4,128)S(1)} all-to-all(f32[64,4,256]{2,1,0:T(4,128)S(1)} %spread.1), channel_id=1, replica_groups=mesh['grp'=2,'dp'=64] {'dp'}, dimensions={0} | all-to-all | bytes 524288 | tf_op jit(solution)/shard_map/all_to_all | solution.py:377
  44.7 3.1 %collective-permute-start.1 = (f32[64,4,256]{2,1,0:T(4,128)S(1)}, f32[64,4,256]{2,1,0:T(4,128)S(1)}, u32[]{:S(2)}, u32[]{:S(2)}) collective-permute-start(f32[64,4,256]{2,1,0:T(4,128)S(1)} %all_to_all.11.mine), channel_id=1, source_target_pairs={{0,64},{64,0},{1,65},{65,1},{2,66},{66,2},{3,67},{67,3},{4,68},{68... | collective-permute-start | bytes 786440 | tf_op jit(solution)/shard_map/ppermute | solution.py:378
  47.8 1.2 %collective-permute-done.1.other = f32[64,4,256]{2,1,0:T(4,128)S(1)} collective-permute-done((f32[64,4,256]{2,1,0:T(4,128)S(1)}, f32[64,4,256]{2,1,0:T(4,128)S(1)}, u32[]{:S(2)}, u32[]{:S(2)}) %collective-permute-start.1) | collective-permute-done | bytes 262176 | tf_op jit(solution)/shard_map/ppermute | solution.py:378
  49.0 1.5 %bases.1 = (f32[5,4,128]{2,1,0:T(4,128)S(1)}, f32[8,128,128]{2,1,0:T(8,128)S(1)}) custom-call(f32[64,4,256]{2,1,0:T(4,128)S(1)} %all_to_all.11.mine, f32[64,4,256]{2,1,0:T(4,128)S(1)} %collective-permute-done.1.other, bf16[32768,128]{1,0:T(8,128)(2,1)S(1)} %get-tuple-element.13.comp), custom_call_target="tpu_custom_call" | custom-call | tf_op jit(solution)/shard_map/bases/pallas_call | solution.py:252
  50.5 0.4 collective-permute-start.2
  50.9 0.1 aside.1
  51.0 0.7 %collective-permute-done.2.q_other = f32[5,4,128]{2,1,0:T(4,128)S(1)} collective-permute-done((f32[5,4,128]{2,1,0:T(4,128)S(1)}, f32[5,4,128]{2,1,0:T(4,128)S(1)}, u32[]{:S(2)}, u32[]{:S(2)}) %collective-permute-start.2) | collective-permute-done | bytes 10272 | tf_op jit(solution)/shard_map/ppermute | solution.py:380
  51.7 3.7 %new_residual.1 = (bf16[1,32768,128]{2,1,0:T(8,128)(2,1)}, f32[5,4,128]{2,1,0:T(4,128)}, f32[1,4,14336]{2,1,0:T(4,128)}) custom-call(f32[5,4,128]{2,1,0:T(4,128)S(1)} %get-tuple-element.14.q_mine, f32[5,4,128]{2,1,0:T(4,128)S(1)} %collective-permute-done.2.q_other, bf16[8,128,128]{2,1,0:T(8,128)(2,1)S(1)} %get-tuple-element.17.turned, ...), custom_call_target="tpu_custom_call" | custom-call | tf_op jit(solution)/shard_map/new_residual/pallas_call | solution.py:353
Async XLA Ops:
  7.2 2.6 %collective-permute-start = (f32[64,4,256]{2,1,0:T(4,128)S(1)}, f32[64,4,256]{2,1,0:T(4,128)S(1)}, u32[]{:S(2)}, u32[]{:S(2)}) collective-permute-start(f32[64,4,256]{2,1,0:T(4,128)S(1)} %get-tuple-element.12), channel_id=1, source_target_pairs={{0,64},{64,0},{1,65},{65,1},{2,66},{66,2},{3,67},{67,3},{4,68},{68... | collective-permute-start | bytes 786440 | tf_op jit(solution)/shard_map/ppermute | solution.py:375
  44.7 4.2 %collective-permute-start.1 = (f32[64,4,256]{2,1,0:T(4,128)S(1)}, f32[64,4,256]{2,1,0:T(4,128)S(1)}, u32[]{:S(2)}, u32[]{:S(2)}) collective-permute-start(f32[64,4,256]{2,1,0:T(4,128)S(1)} %all_to_all.11.mine), channel_id=1, source_target_pairs={{0,64},{64,0},{1,65},{65,1},{2,66},{66,2},{3,67},{67,3},{4,68},{68... | collective-permute-start | bytes 786440 | tf_op jit(solution)/shard_map/ppermute | solution.py:378
  50.5 1.3 %collective-permute-start.2 = (f32[5,4,128]{2,1,0:T(4,128)S(1)}, f32[5,4,128]{2,1,0:T(4,128)S(1)}, u32[]{:S(2)}, u32[]{:S(2)}) collective-permute-start(f32[5,4,128]{2,1,0:T(4,128)S(1)} %get-tuple-element.14.q_mine), channel_id=1, source_target_pairs={{0,64},{64,0},{1,65},{65,1},{2,66},{66,2},{3,67},{67,3},{4,68},{68... | collective-permute-start | bytes 30728 | tf_op jit(solution)/shard_map/ppermute | solution.py:380
